TPU v7x, 32 devices: a 4x4x1 block of a 4x4x8 slice. The times are simulated.
32 devices in a mesh: dp: 1 (over z), sp: 32 (over y, x, core).
Axes of the slice: x: 4, y: 4, z: 1, core: 2. Of those that a mesh axis runs over, the one named last changes fastest.
The devices are a block of a 4x4x8 slice.
Arguments:
- x_one: bfloat16 [1024, 5120], P(('dp', 'sp'))
- seg_one: int32 [1024], P(('dp', 'sp'))
- pos_one: int32 [1024], P(('dp', 'sp'))
- x_two: bfloat16 [1024, 5120], P(('dp', 'sp'))
- seg_two: int32 [1024], P(('dp', 'sp'))
- pos_two: int32 [1024], P(('dp', 'sp'))
- w_qdown: bfloat16 [5120, 1536], replicated
- gain_q: bfloat16 [1536], replicated
- w_qup: bfloat16 [1536, 24576], replicated
- w_kvdown: bfloat16 [5120, 576], replicated
- gain_kv: bfloat16 [512], replicated
- w_kvup: bfloat16 [512, 32768], replicated
- w_out: bfloat16 [16384, 5120], replicated
Outputs:
- output 1: bfloat16 [1024, 5120], P(('dp', 'sp'))
- output 2: bfloat16 [1024, 5120], P(('dp', 'sp'))
All inputs are finite; a program needn't handle non-finite values.
Results may differ from a plain program's by a relative error of at most 0.0140873.
Values are sent between devices in bfloat16 or wider.
A program may use at most 768 MiB of HBM per device.

v0:
```python
import jax
import jax.numpy as jnp
from jax import lax
from jax.sharding import PartitionSpec as P

NOPE_DIM = 128
ROPE_DIM = 64
KV_LAT = 512
V_DIM = 128
QK_DIM = NOPE_DIM + ROPE_DIM
ROPE_BASE = 10000.0
NORM_EPS = 1e-6


def rms_scale(pre_norm, gain_vec):
    mean_sq = jnp.mean(pre_norm * pre_norm, axis=-1, keepdims=True)
    return (pre_norm * lax.rsqrt(mean_sq + NORM_EPS) * gain_vec.astype(jnp.float32)).astype(jnp.bfloat16)


def rope_tables(positions):
    half_dim = ROPE_DIM // 2
    inv_freq = ROPE_BASE ** (-jnp.arange(half_dim, dtype=jnp.float32) / half_dim)
    angles = positions.astype(jnp.float32)[..., None] * inv_freq
    return jnp.cos(angles), jnp.sin(angles)


def rope_rotate(rot_in, cos_tab, sin_tab):
    half_dim = ROPE_DIM // 2
    first_half = rot_in[..., :half_dim]
    second_half = rot_in[..., half_dim:]
    return jnp.concatenate([first_half * cos_tab - second_half * sin_tab, second_half * cos_tab + first_half * sin_tab], axis=-1)


def latent_stage(x_local, pos_local, w_qdown, gain_q, w_kvdown, gain_kv):
    q_latent = rms_scale(jnp.dot(x_local, w_qdown, preferred_element_type=jnp.float32), gain_q)
    kv_raw = jnp.dot(x_local, w_kvdown, preferred_element_type=jnp.float32)
    kv_latent = rms_scale(kv_raw[:, :KV_LAT], gain_kv)
    cos_tab, sin_tab = rope_tables(pos_local)
    k_rope = rope_rotate(kv_raw[:, KV_LAT:], cos_tab, sin_tab).astype(jnp.bfloat16)
    return q_latent, kv_latent, k_rope


def head_attention(q_latent, kv_latent, k_rope, prompt_ids, positions, w_qup_cols, w_kvup_cols):
    num_tok = q_latent.shape[0]
    q_full = jnp.dot(q_latent, w_qup_cols, preferred_element_type=jnp.float32).reshape(num_tok, -1, QK_DIM)
    cos_tab, sin_tab = rope_tables(positions)
    q_nope = q_full[..., :NOPE_DIM].astype(jnp.bfloat16)
    q_rope = rope_rotate(q_full[..., NOPE_DIM:], cos_tab[:, None], sin_tab[:, None]).astype(jnp.bfloat16)
    kv_full = jnp.dot(kv_latent, w_kvup_cols, preferred_element_type=jnp.float32).astype(jnp.bfloat16).reshape(num_tok, -1, NOPE_DIM + V_DIM)
    scores = jnp.einsum('qhd,khd->hqk', q_nope, kv_full[..., :NOPE_DIM], preferred_element_type=jnp.float32)
    scores = scores + jnp.einsum('qhr,kr->hqk', q_rope, k_rope, preferred_element_type=jnp.float32)
    allowed = (prompt_ids[:, None] == prompt_ids[None, :]) & (positions[None, :] <= positions[:, None])
    attn_prob = jax.nn.softmax(jnp.where(allowed[None], scores * QK_DIM ** -0.5, -1e30), axis=-1).astype(jnp.bfloat16)
    return jnp.einsum('hqk,khv->qhv', attn_prob, kv_full[..., NOPE_DIM:], preferred_element_type=jnp.float32).astype(jnp.bfloat16)


def solution(mesh):
    tok_spec = P(('dp', 'sp'), None)
    idx_spec = P(('dp', 'sp'))
    col_spec = P(None, 'sp')

    def micro_block(x_local, seg_local, pos_local, w_qdown, gain_q, w_qup_cols, w_kvdown, gain_kv, w_kvup_cols, w_out):
        q_latent, kv_latent, k_rope = latent_stage(x_local, pos_local, w_qdown, gain_q, w_kvdown, gain_kv)
        q_all = lax.all_gather(q_latent, 'sp', axis=0, tiled=True)
        kv_all = lax.all_gather(kv_latent, 'sp', axis=0, tiled=True)
        rope_all = lax.all_gather(k_rope, 'sp', axis=0, tiled=True)
        seg_all = lax.all_gather(seg_local, 'sp', axis=0, tiled=True)
        pos_all = lax.all_gather(pos_local, 'sp', axis=0, tiled=True)
        head_out = head_attention(q_all, kv_all, rope_all, seg_all, pos_all, w_qup_cols, w_kvup_cols)
        tok_out = lax.all_to_all(head_out, 'sp', 0, 1, tiled=True)
        attn_flat = tok_out.reshape(tok_out.shape[0], -1)
        return jnp.dot(attn_flat, w_out, preferred_element_type=jnp.float32).astype(jnp.bfloat16)

    def local_body(x_one, seg_one, pos_one, x_two, seg_two, pos_two, w_qdown, gain_q, w_qup_cols, w_kvdown, gain_kv, w_kvup_cols, w_out):
        y_one = micro_block(x_one, seg_one, pos_one, w_qdown, gain_q, w_qup_cols, w_kvdown, gain_kv, w_kvup_cols, w_out)
        y_two = micro_block(x_two, seg_two, pos_two, w_qdown, gain_q, w_qup_cols, w_kvdown, gain_kv, w_kvup_cols, w_out)
        return y_one, y_two

    return jax.shard_map(local_body, mesh=mesh, in_specs=(tok_spec, idx_spec, idx_spec, tok_spec, idx_spec, idx_spec, P(), P(), col_spec, P(), P(), col_spec, P()), out_specs=(tok_spec, tok_spec), check_vma=False)
```

profile of v0, /device:TPU:97, one launch (start us, length us, event | category | flops | bytes accessed | tf_op | source)
XLA Modules:
  0.0 414.0 jit_solution(10661553752647034768)
XLA Ops:
  7.3 4.6 %fusion.58 = f32[32,576]{1,0:T(8,128)S(1)} fusion(bf16[32,5120]{1,0:T(8,128)(2,1)} %param.13, bf16[5120,576]{0,1:T(8,128)(2,1)} %param.22), kind=kOutput, calls=%fused_computation.99 | convolution fusion | flops 188743680 | bytes 6299648 | tf_op jit(solution)/shard_map/dot_general | solution.py:36
  11.9 4.5 %fusion.59 = f32[32,576]{1,0:T(8,128)S(1)} fusion(bf16[32,5120]{1,0:T(8,128)(2,1)S(1)} %copy-done, bf16[5120,576]{0,1:T(8,128)(2,1)} %param.22), kind=kOutput, calls=%fused_computation.100 | convolution fusion | flops 188743680 | bytes 6299648 | tf_op jit(solution)/shard_map/dot_general | solution.py:36
  19.1 8.3 %multiply_reduce_fusion = (f32[32]{0:T(128)S(1)}, f32[32,1536]{1,0:T(8,128)S(1)}) fusion(bf16[32,5120]{1,0:T(8,128)(2,1)S(1)} %copy-done, bf16[5120,1536]{1,0:T(8,128)(2,1)} %param.19), kind=kOutput, calls=%fused_computation.51 | convolution fusion | flops 503414752 | bytes 16253056 | tf_op jit(solution)/shard_map/dot_general | solution.py:35
  27.4 8.3 %multiply_reduce_fusion.1 = (f32[32]{0:T(128)S(1)}, f32[32,1536]{1,0:T(8,128)S(1)}) fusion(bf16[32,5120]{1,0:T(8,128)(2,1)S(1)} %copy-done.2, bf16[5120,1536]{1,0:T(8,128)(2,1)} %param.19), kind=kOutput, calls=%fused_computation.53 | convolution fusion | flops 503414752 | bytes 16253056 | tf_op jit(solution)/shard_map/dot_general | solution.py:35
  38.2 50.1 %all-reduce.4 = (s32[1024]{0:T(1024)S(1)}, s32[1024]{0:T(1024)S(1)}, s32[1024]{0:T(1024)S(1)}, s32[1024]{0:T(1024)S(1)}) all-reduce(s32[1024]{0:T(1024)S(1)} %dynamic-update-slice.1, s32[1024]{0:T(1024)S(1)} %dynamic-update-slice, s32[1024]{0:T(1024)S(1)} %dynamic-update-slice.3, ...), channel_id=1, replica_groups=mesh['dp'=1,'sp'=32] {'sp'}, use_global_device_ids=true, to_apply=%add.1 | all-reduce | flops 4096 | bytes 32768
  88.6 27.9 %all_gather.39 = bf16[1024,64]{1,0:T(8,128)(2,1)S(1)} all-gather(bf16[32,64]{1,0:T(8,128)(2,1)S(1)} %pad_maximum_fusion.1), channel_id=1, replica_groups=mesh['dp'=1,'sp'=32] {'sp'}, dimensions={0}, use_global_device_ids=true | all-gather | bytes 135168 | tf_op jit(solution)/shard_map/all_gather | solution.py:66
  116.6 33.2 %all_gather.34 = bf16[1024,64]{1,0:T(8,128)(2,1)S(1)} all-gather(bf16[32,64]{1,0:T(8,128)(2,1)S(1)} %pad_maximum_fusion), channel_id=1, replica_groups=mesh['dp'=1,'sp'=32] {'sp'}, dimensions={0}, use_global_device_ids=true | all-gather | bytes 135168 | tf_op jit(solution)/shard_map/all_gather | solution.py:66
  153.4 4.2 %convolution_convert_fusion.2 = bf16[1024,1024]{0,1:T(8,128)(2,1)} fusion(bf16[1024,512]{1,0:T(8,128)(2,1)} %all-gather.9.cloned.1.call-done, bf16[512,32768]{1,0:T(8,128)(2,1)} %param.24, s32[]{:T(128)S(6)} %multiply.30), kind=kOutput, calls=%fused_computation.24 | convolution fusion | flops 1074790400 | bytes 4194308 | tf_op jit(solution)/shard_map/dot_general | solution.py:49
  157.6 4.2 %convolution_convert_fusion.3 = bf16[1024,1024]{0,1:T(8,128)(2,1)} fusion(bf16[1024,512]{1,0:T(8,128)(2,1)} %all-gather.5.cloned.1.call-done, bf16[512,32768]{1,0:T(8,128)(2,1)} %param.24, s32[]{:T(128)S(6)} %multiply.30), kind=kOutput, calls=%fused_computation.25 | convolution fusion | flops 1074790400 | bytes 4194308 | tf_op jit(solution)/shard_map/dot_general | solution.py:49
  161.8 5.5 %fusion.8 = f32[1024,768]{0,1:T(8,128)S(1)} fusion(bf16[1024,1536]{1,0:T(8,128)(2,1)} %all-gather.11.cloned.1.call-done, bf16[1536,24576]{1,0:T(8,128)(2,1)} %param.21, s32[]{:T(128)S(6)} %multiply.32), kind=kOutput, calls=%fused_computation.20 | convolution fusion | flops 2415919104 | bytes 8650756 | tf_op jit(solution)/shard_map/dot_general | solution.py:45
  167.5 8.0 %fusion.26 = f32[1024,1024,4]{1,0,2:T(8,128)} fusion(bf16[1024,4,32]{0,2,1:T(8,128)(2,1)S(1)} %get-tuple-element.7, bf16[1024,4,32]{0,2,1:T(8,128)(2,1)S(1)} %get-tuple-element.6, bf16[1024,64]{1,0:T(8,128)(2,1)S(1)} %all_gather.39), kind=kOutput, calls=%fused_computation.40 | convolution fusion | flops 537919488 | bytes 17432576 | tf_op jit(solution)/shard_map/qhr,kr->hqk/dot_general | solution.py:51
  175.5 11.1 %fusion.3 = f32[4,1024,1024]{1,2,0:T(8,128)} fusion(f32[1024,1024,4]{1,0,2:T(8,128)} %fusion.26, pred[1024,1024]{0,1:T(8,128)(4,1)S(1)} %compare_and_fusion, f32[1024,4,192]{0,2,1:T(8,128)S(1)} %bitcast.57, bf16[1024,4,256]{0,2,1:T(8,128)(2,1)S(1)} %bitcast.61), kind=kOutput, calls=%fused_computation.4 | convolution fusion | flops 1086324736 | bytes 36700160 | tf_op jit(solution)/shard_map/qhd,khd->hqk/dot_general | solution.py:50
  186.6 12.1 %fusion.57 = f32[4,1024]{1,0:T(4,128)S(1)} fusion(f32[4,1024,1024]{1,2,0:T(8,128)} %fusion.3), kind=kOutput, calls=%fused_computation.98 | output fusion | flops 8389631 | bytes 16793600 | tf_op jit(solution)/shard_map/sub | solution.py:53
  198.7 13.0 %fusion.15 = bf16[1024,4,128]{0,2,1:T(8,128)(2,1)S(1)} fusion(f32[4,1024]{1,0:T(4,128)S(1)} %fusion.57, bf16[1024,4,256]{0,2,1:T(8,128)(2,1)} %bitcast.60, f32[4,1024,1024]{1,2,0:T(8,128)} %fusion.3), kind=kOutput, calls=%fused_computation.29 | convolution fusion | flops 1086854144 | bytes 35667968 | tf_op jit(solution)/shard_map/hqk,khv->qhv/dot_general | solution.py:54
  213.1 10.2 %all-to-all-start.1 = ((bf16[1024,4,128]{2,1,0:T(4,128)(2,1)}), bf16[1024,4,128]{2,1,0:T(4,128)(2,1)S(1)}, u32[]{:S(2)}, u32[]{:S(2)}) async-start(bf16[1024,4,128]{2,1,0:T(4,128)(2,1)} %copy.52), calls=%async_computation.1 | async-start | bytes 2097152 | tf_op jit(solution)/shard_map/all_to_all | solution.py:70
  223.3 5.5 %fusion.10 = f32[1024,768]{0,1:T(8,128)S(1)} fusion(bf16[1024,1536]{1,0:T(8,128)(2,1)} %all-gather.7.cloned.1.call-done, bf16[1536,24576]{1,0:T(8,128)(2,1)} %param.21, s32[]{:T(128)S(6)} %multiply.32), kind=kOutput, calls=%fused_computation.22 | convolution fusion | flops 2415919104 | bytes 8650756 | tf_op jit(solution)/shard_map/dot_general | solution.py:45
  229.0 8.0 %fusion.22 = f32[1024,1024,4]{1,0,2:T(8,128)} fusion(bf16[1024,4,32]{0,2,1:T(8,128)(2,1)S(1)} %get-tuple-element.9, bf16[1024,4,32]{0,2,1:T(8,128)(2,1)S(1)} %get-tuple-element.8, bf16[1024,64]{1,0:T(8,128)(2,1)S(1)} %all_gather.34), kind=kOutput, calls=%fused_computation.36 | convolution fusion | flops 537919488 | bytes 17432576 | tf_op jit(solution)/shard_map/qhr,kr->hqk/dot_general | solution.py:51
  237.0 11.1 %fusion.5 = f32[4,1024,1024]{1,2,0:T(8,128)} fusion(f32[1024,1024,4]{1,0,2:T(8,128)} %fusion.22, pred[1024,1024]{0,1:T(8,128)(4,1)S(1)} %compare_and_fusion.1, f32[1024,4,192]{0,2,1:T(8,128)S(1)} %bitcast.55, bf16[1024,4,256]{0,2,1:T(8,128)(2,1)S(1)} %bitcast.59), kind=kOutput, calls=%fused_computation.7 | convolution fusion | flops 1086324736 | bytes 36700160 | tf_op jit(solution)/shard_map/qhd,khd->hqk/dot_general | solution.py:50
  248.1 12.1 %fusion.56 = f32[4,1024]{1,0:T(4,128)S(1)} fusion(f32[4,1024,1024]{1,2,0:T(8,128)} %fusion.5), kind=kOutput, calls=%fused_computation.97 | output fusion | flops 8389631 | bytes 16793600 | tf_op jit(solution)/shard_map/sub | solution.py:53
  260.1 13.0 %fusion.14 = bf16[1024,4,128]{0,2,1:T(8,128)(2,1)S(1)} fusion(f32[4,1024]{1,0:T(4,128)S(1)} %fusion.56, bf16[1024,4,256]{0,2,1:T(8,128)(2,1)} %bitcast.58, f32[4,1024,1024]{1,2,0:T(8,128)} %fusion.5), kind=kOutput, calls=%fused_computation.28 | convolution fusion | flops 1086854144 | bytes 35667968 | tf_op jit(solution)/shard_map/hqk,khv->qhv/dot_general | solution.py:54
  274.6 7.0 %all-to-all-start = ((bf16[1024,4,128]{2,1,0:T(4,128)(2,1)}), bf16[1024,4,128]{2,1,0:T(4,128)(2,1)S(1)}, u32[]{:S(2)}, u32[]{:S(2)}) async-start(bf16[1024,4,128]{2,1,0:T(4,128)(2,1)} %copy.46), calls=%async_computation | async-start | bytes 2097152 | tf_op jit(solution)/shard_map/all_to_all | solution.py:70
  283.4 14.1 %all-to-all-done = bf16[1024,4,128]{2,1,0:T(4,128)(2,1)S(1)} async-done(((bf16[1024,4,128]{2,1,0:T(4,128)(2,1)}), bf16[1024,4,128]{2,1,0:T(4,128)(2,1)S(1)}, u32[]{:S(2)}, u32[]{:S(2)}) %all-to-all-start) | async-done | bytes 1048608 | tf_op jit(solution)/shard_map/all_to_all | solution.py:70
  299.2 53.9 %convolution_convert_fusion = bf16[32,5120]{1,0:T(8,128)(2,1)} fusion(bf16[32,16384]{1,0:T(8,128)(2,1)S(1)} %reshape.277, bf16[16384,5120]{1,0:T(8,128)(2,1)} %param.25), kind=kOutput, calls=%fused_computation.14 | convolution fusion | flops 5368872960 | bytes 169148416 | tf_op jit(solution)/shard_map/dot_general | solution.py:72
  353.1 53.9 %convolution_convert_fusion.1 = bf16[32,5120]{1,0:T(8,128)(2,1)} fusion(bf16[32,16384]{1,0:T(8,128)(2,1)S(1)} %reshape.274, bf16[16384,5120]{1,0:T(8,128)(2,1)} %param.25), kind=kOutput, calls=%fused_computation.15 | convolution fusion | flops 5368872960 | bytes 169148416 | tf_op jit(solution)/shard_map/dot_general | solution.py:72
  (70 shorter events, 15.8 us)
Async XLA Ops:
  7.2 4.7 %copy-start = (bf16[32,5120]{1,0:T(8,128)(2,1)S(1)}, bf16[32,5120]{1,0:T(8,128)(2,1)}, u32[]{:S(2)}) copy-start(bf16[32,5120]{1,0:T(8,128)(2,1)} %param.16) | copy-start | bytes 983044
  7.2 146.2 %all-gather.9.cloned.1.call-start = ((), (), s32[]{:S(2)}) async-start(), calls=%async_computation.4 | async-start | bytes 1081344 | tf_op jit(solution)/shard_map/all_gather | solution.py:65
  11.9 15.4 %copy-start.5 = (bf16[1536]{0:T(1024)(128)(2,1)S(1)}, bf16[1536]{0:T(1024)(128)(2,1)}, u32[]{:S(2)}) copy-start(bf16[1536]{0:T(1024)(128)(2,1)} %param.20) | copy-start | bytes 9220
  11.9 15.5 %copy-start.2 = (bf16[32,5120]{1,0:T(8,128)(2,1)S(1)}, bf16[32,5120]{1,0:T(8,128)(2,1)}, u32[]{:S(2)}) copy-start(bf16[32,5120]{1,0:T(8,128)(2,1)} %param.13) | copy-start | bytes 983044
  18.2 139.5 %all-gather.5.cloned.1.call-start = ((), (), s32[]{:S(2)}) async-start(), calls=%async_computation.2 | async-start | bytes 1081344 | tf_op jit(solution)/shard_map/all_gather | solution.py:65
  19.0 142.8 %all-gather.11.cloned.1.call-start = ((), (), s32[]{:S(2)}) async-start(), calls=%async_computation.5 | async-start | bytes 3244032 | tf_op jit(solution)/shard_map/all_gather | solution.py:64
  27.3 9.9 %copy-start.6 = (s32[32]{0:T(128)S(1)}, s32[32]{0:T(128)}, u32[]{:S(2)}) copy-start(s32[32]{0:T(128)} %param.15) | copy-start | bytes 388
  27.4 9.9 %copy-start.7 = (s32[32]{0:T(128)S(1)}, s32[32]{0:T(128)}, u32[]{:S(2)}) copy-start(s32[32]{0:T(128)} %param.18) | copy-start | bytes 388
  27.4 10.3 %copy-start.8 = (s32[32]{0:T(128)S(1)}, s32[32]{0:T(128)}, u32[]{:S(2)}) copy-start(s32[32]{0:T(128)} %param.14) | copy-start | bytes 388
  27.4 10.6 %copy-start.9 = (s32[32]{0:T(128)S(1)}, s32[32]{0:T(128)}, u32[]{:S(2)}) copy-start(s32[32]{0:T(128)} %param.17) | copy-start | bytes 388
  36.5 186.8 %all-gather.7.cloned.1.call-start = ((), (), s32[]{:S(2)}) async-start(), calls=%async_computation.3 | async-start | bytes 3244032 | tf_op jit(solution)/shard_map/all_gather | solution.py:64
  161.8 13.7 %copy-start.4 = (bf16[1024,1024]{0,1:T(8,128)(2,1)S(1)}, bf16[1024,1024]{0,1:T(8,128)(2,1)}, u32[]{:S(2)}) copy-start(bf16[1024,1024]{0,1:T(8,128)(2,1)} %convolution_convert_fusion.2) | copy-start | bytes 6291460
  213.1 61.5 %all-to-all-start.1 = ((bf16[1024,4,128]{2,1,0:T(4,128)(2,1)}), bf16[1024,4,128]{2,1,0:T(4,128)(2,1)S(1)}, u32[]{:S(2)}, u32[]{:S(2)}) async-start(bf16[1024,4,128]{2,1,0:T(4,128)(2,1)} %copy.52), calls=%async_computation.1 | async-start | bytes 2097152 | tf_op jit(solution)/shard_map/all_to_all | solution.py:70
  223.3 13.7 %copy-start.3 = (bf16[1024,1024]{0,1:T(8,128)(2,1)S(1)}, bf16[1024,1024]{0,1:T(8,128)(2,1)}, u32[]{:S(2)}) copy-start(bf16[1024,1024]{0,1:T(8,128)(2,1)} %convolution_convert_fusion.3) | copy-start | bytes 6291460
  274.6 22.9 %all-to-all-start = ((bf16[1024,4,128]{2,1,0:T(4,128)(2,1)}), bf16[1024,4,128]{2,1,0:T(4,128)(2,1)S(1)}, u32[]{:S(2)}, u32[]{:S(2)}) async-start(bf16[1024,4,128]{2,1,0:T(4,128)(2,1)} %copy.46), calls=%async_computation | async-start | bytes 2097152 | tf_op jit(solution)/shard_map/all_to_all | solution.py:70
  353.1 53.9 %copy-start.1 = (bf16[32,5120]{1,0:T(8,128)(2,1)S(1)}, bf16[32,5120]{1,0:T(8,128)(2,1)}, u32[]{:S(2)}) copy-start(bf16[32,5120]{1,0:T(8,128)(2,1)} %param.16) | copy-start | bytes 983044
Sparse Core Ops, SparseCore 0:
  18.3 41.7 all-gather.8
  62.2 36.6 all-gather.4
  101.6 39.4 all-gather.10
  143.6 38.9 all-gather.6
where the time goes:
time: 421 us; the launch traced here: 414 us
  matrix products  217 us (52%)
  blocking collectives  111 us (26%)
  other arithmetic  30.8 us (7%)
  starting transfers between devices  17.4 us (4%)
  waiting for transfers between devices  15.5 us (4%)
  between operations  14.5 us (3%)
  local copies, waits for them, and re-layouts  7.42 us (2%)
    dot_general x2, matrix products, micro_block(): jnp.dot(attn_flat, w_out, preferred_element_type=jnp.float32)  108 us
    all_gather x2, blocking collectives, micro_block(): rope_all = lax.all_gather(k_rope, 'sp', axis=0, tiled=True)  61.2 us
    unnamed x1, blocking collectives  50.1 us
    dot_general x2, matrix products, head_attention(): jnp.einsum('hqk,khv->qhv', attn_prob, kv_full[..., NOPE_DIM:], preferred_...  26 us
    sub x2, other arithmetic, head_attention(): jax.nn.softmax(jnp.where(allowed[None], scores * QK_DIM ** (-0.5), -1e+30...  24.1 us
    dot_general x2, matrix products, head_attention(): jnp.einsum('qhd,khd->hqk', q_nope, kv_full[..., :NOPE_DIM], preferred_ele...  22.1 us
    all_to_all x2, starting transfers between devices, micro_block(): tok_out = lax.all_to_all(head_out, 'sp', 0, 1, tiled=True)  17.1 us
    dot_general x2, matrix products, latent_stage(): jnp.dot(x_local, w_qdown, preferred_element_type=jnp.float32)  16.5 us
  transfers between devices with their start and end apart: 6, of which 1 were waited for; matrix products, arithmetic and copies ran while one was open for 33% of the time, Pallas kernels for 0%

commit v1 on v0

v1 whole, which is shorter than its diff:
```python
import functools

import jax
import jax.numpy as jnp
from jax import lax
from jax.experimental import pallas as pl
from jax.experimental.pallas import tpu as pltpu
from jax.sharding import PartitionSpec as P

NOPE_DIM = 128
ROPE_DIM = 64
KV_LAT = 512
V_DIM = 128
QK_DIM = NOPE_DIM + ROPE_DIM
KV_HEAD = NOPE_DIM + V_DIM
ROPE_BASE = 10000.0
NORM_EPS = 1e-6
LANES = 128

CORES = 2
ROW = 4
X_BIT = CORES
Y_BIT = CORES * ROW
CHIP_MASKS = (0, X_BIT, Y_BIT, X_BIT + Y_BIT)
CHIPS = len(CHIP_MASKS)
MEMBERS = CHIPS * CORES
MICRO = 2
KV_PACK = KV_LAT + LANES
HEADS_PER_STEP = 2
CHUNKS = 2
VMEM_LIMIT = 60 * 1024 * 1024
MESH = pl.DeviceIdType.MESH


def rms_scale(pre_norm, gain_vec):
    mean_sq = jnp.mean(pre_norm * pre_norm, axis=-1, keepdims=True)
    return (pre_norm * lax.rsqrt(mean_sq + NORM_EPS) * gain_vec.astype(jnp.float32)).astype(jnp.bfloat16)


def rope_tables(positions):
    half_dim = ROPE_DIM // 2
    inv_freq = ROPE_BASE ** (-jnp.arange(half_dim, dtype=jnp.float32) / half_dim)
    angles = positions.astype(jnp.float32)[..., None] * inv_freq
    return jnp.cos(angles), jnp.sin(angles)


def rope_rotate(rot_in, cos_tab, sin_tab):
    half_dim = ROPE_DIM // 2
    first_half = rot_in[..., :half_dim]
    second_half = rot_in[..., half_dim:]
    return jnp.concatenate([first_half * cos_tab - second_half * sin_tab, second_half * cos_tab + first_half * sin_tab], axis=-1)


def gather_kernel(cq_ref, kv_ref, cq_all, kv_all, loc, cq_send, cq_recv, kv_send, kv_recv):
    me = lax.axis_index("sp")
    core = me % CORES
    chip = me // CORES
    x = chip % ROW
    y = chip // ROW
    flip_x = (1 - 2 * (x % 2))
    flip_y = (1 - 2 * (y % 2))
    sib = me + 1 - 2 * core

    def dev(dy, dx):
        return (((y + dy + ROW) % ROW) * ROW + (x + dx + ROW) % ROW) * CORES + core

    def near(first, second):
        return dev(core * first + (1 - core) * second, (1 - core) * first + core * second)

    px = dev(0, flip_x)
    py = dev(flip_y, 0)
    pd = dev(flip_y, flip_x)
    square = (me, px, py, pd)

    barrier = pltpu.get_barrier_semaphore()
    peers = [sib, pd, near(1, 0), near(-1, 0), near(0, 1), near(0, -1)]
    for peer in peers:
        pl.semaphore_signal(barrier, inc=1, device_id={"sp": peer}, device_id_type=MESH)
    pl.semaphore_wait(barrier, len(peers))

    started = []

    def send(src, dst, sems, to):
        copy = pltpu.make_async_remote_copy(
            src_ref=src, dst_ref=dst, send_sem=sems[0], recv_sem=sems[1], device_id={"sp": to}, device_id_type=MESH
        )
        copy.start()
        started.append(copy)
        return copy

    own_cq = pltpu.make_async_copy(cq_ref, cq_all.at[0, 0], loc.at[0])
    own_kv = pltpu.make_async_copy(kv_ref, kv_all.at[me], loc.at[1])
    own_cq.start()
    own_kv.start()

    cq_in = {}
    for slot in (1, 2, 3):
        cq_in[slot] = send(cq_ref, cq_all.at[slot, 0], (cq_send.at[slot], cq_recv.at[slot]), square[slot])
    send(cq_ref, cq_all.at[0, 1], (cq_send.at[CHIPS], cq_recv.at[CHIPS]), sib)

    n_kv = [0]

    def kv_sems():
        s = n_kv[0]
        n_kv[0] += 1
        return kv_send.at[s], kv_recv.at[s]

    def kv_copy(src_local, owner, to, part=None):
        if part is None:
            src = kv_ref if src_local else kv_all.at[owner]
            return send(src, kv_all.at[owner], kv_sems(), to)
        src = kv_ref.at[part] if src_local else kv_all.at[owner, part]
        return send(src, kv_all.at[owner, part], kv_sems(), to)

    right1, left1 = near(1, 0), near(-1, 0)
    right2, left2 = near(0, 1), near(0, -1)

    first_r = kv_copy(True, me, right1)
    first_l = kv_copy(True, me, left1)

    def second_start(owner, local, part=None):
        r = kv_copy(local, owner, right2, part)
        l = kv_copy(local, owner, left2, part)
        return r, l

    def second_own(f):
        return near(f, 0)

    pairs = [(0, second_start(me, True))]
    d2d = [kv_copy(True, me, sib)]
    first_r.wait_recv()
    fwd_r = kv_copy(False, near(-1, 0), right1, 0)
    pairs.append((-1, second_start(near(-1, 0), False)))
    d2d.append(kv_copy(False, near(-1, 0), sib))
    first_l.wait_recv()
    fwd_l = kv_copy(False, near(1, 0), left1, 1)
    pairs.append((1, second_start(near(1, 0), False)))
    d2d.append(kv_copy(False, near(1, 0), sib))

    for slot in (1, 2, 3):
        cq_in[slot].wait_recv()
        send(cq_all.at[slot, 0], cq_all.at[slot, 1], (cq_send.at[CHIPS + slot], cq_recv.at[CHIPS + slot]), sib)

    fwd_r.wait_recv()
    fwd_l.wait_recv()
    far = near(2, 0)
    pairs.append((2, second_start(far, False)))
    d2d.append(kv_copy(False, far, sib))

    tail = []
    for f, (r, l) in pairs:
        r.wait_recv()
        tail.append((f, kv_copy(False, near(f, -1), right2, 0), None))
        d2d.append(kv_copy(False, near(f, -1), sib))
        l.wait_recv()
        tail.append((f, kv_copy(False, near(f, 1), left2, 1), None))
        d2d.append(kv_copy(False, near(f, 1), sib))
    for i in range(0, len(tail), 2):
        f = tail[i][0]
        tail[i][1].wait_recv()
        tail[i + 1][1].wait_recv()
        d2d.append(kv_copy(False, near(f, 2), sib))

    for copy in d2d:
        copy.wait_recv()
    for copy in started:
        if copy is started[3]:
            copy.wait_recv()
    for slot in (1, 2, 3):
        pltpu.make_async_remote_copy(
            src_ref=cq_all.at[slot, 0],
            dst_ref=cq_all.at[slot, 1],
            send_sem=cq_send.at[CHIPS + slot],
            recv_sem=cq_recv.at[CHIPS + slot],
            device_id={"sp": sib},
            device_id_type=MESH,
        ).wait_recv()
    for copy in started:
        copy.wait_send()
    own_cq.wait()
    own_kv.wait()


def gather_latents(cq, kv, group):
    n_kv = 2 + 2 + 4 * 2 + 4 * 2 + group // CORES
    return pl.pallas_call(
        gather_kernel,
        out_shape=(
            jax.ShapeDtypeStruct((CHIPS, CORES) + cq.shape, cq.dtype),
            jax.ShapeDtypeStruct((group,) + kv.shape, kv.dtype),
        ),
        in_specs=[pl.BlockSpec(memory_space=pltpu.VMEM)] * 2,
        out_specs=(pl.BlockSpec(memory_space=pltpu.VMEM),) * 2,
        scratch_shapes=[
            pltpu.SemaphoreType.DMA((2,)),
            pltpu.SemaphoreType.DMA((2 * CHIPS,)),
            pltpu.SemaphoreType.DMA((2 * CHIPS,)),
            pltpu.SemaphoreType.DMA((n_kv,)),
            pltpu.SemaphoreType.DMA((n_kv,)),
        ],
        compiler_params=pltpu.CompilerParams(collective_id=0, has_side_effects=True, vmem_limit_bytes=VMEM_LIMIT),
        name="gather_latents",
    )(cq, kv)


def attention_kernel(first_pair, cq_ref, kv_ref, wq_ref, wkv_ref, cos_ref, sin_ref, qlo_ref, qhi_ref, kcode_ref, o0, o1, o2, o3, kcat_ref, v_ref, mask_ref):
    del first_pair
    outs = (o0, o1, o2, o3)
    dev, _, rows, q_lat = cq_ref.shape[1:] if False else (kv_ref.shape[0], None, kv_ref.shape[2], cq_ref.shape[-1])
    keys = dev * rows
    q_rows = MEMBERS * rows

    @pl.when(pl.program_id(0) == 0)
    def _():
        for mb in range(MICRO):
            kcat_ref[mb, :, NOPE_DIM:] = kv_ref[:, mb, :, KV_LAT:].reshape(keys, LANES)
            code = kcode_ref[mb]
            keep = (code >= qlo_ref[mb]) & (code <= qhi_ref[mb])
            mask_ref[mb] = jnp.where(keep, 1.0, 0.0)

    cq = cq_ref[...].reshape(MEMBERS * MICRO * rows, q_lat)
    latent = kv_ref[...].reshape(dev * MICRO * rows, KV_PACK)[:, :KV_LAT]
    for hh in range(HEADS_PER_STEP):
        kv = jnp.dot(latent, wkv_ref[:, hh * KV_HEAD:(hh + 1) * KV_HEAD], preferred_element_type=jnp.float32)
        kv = kv.astype(jnp.bfloat16).reshape(dev, MICRO, rows, KV_HEAD)
        for mb in range(MICRO):
            one = kv[:, mb].reshape(keys, KV_HEAD)
            kcat_ref[mb, :, :NOPE_DIM] = one[:, :NOPE_DIM]
            v_ref[mb] = one[:, NOPE_DIM:]
        f = jnp.dot(cq, wq_ref[:, hh * QK_DIM:(hh + 1) * QK_DIM], preferred_element_type=jnp.float32)
        z = f[:, NOPE_DIM:]
        turned = jnp.concatenate([z[:, ROPE_DIM // 2:], z[:, :ROPE_DIM // 2]], axis=1)
        rot = z * cos_ref[...] + turned * sin_ref[...]
        pad = jnp.zeros((rot.shape[0], LANES - ROPE_DIM), jnp.float32)
        q = jnp.concatenate([f[:, :NOPE_DIM], rot, pad], axis=1).astype(jnp.bfloat16)
        q = q.reshape(MEMBERS, MICRO, rows, NOPE_DIM + LANES)
        for mb in range(MICRO):
            s = lax.dot_general(
                q[:, mb].reshape(q_rows, NOPE_DIM + LANES), kcat_ref[mb], (((1,), (1,)), ((), ())), preferred_element_type=jnp.float32
            )
            s = jnp.where(mask_ref[mb] > 0.5, s * QK_DIM ** -0.5, -1e30)
            e = jnp.exp(s - jnp.max(s, axis=1, keepdims=True))
            p = (e * (1.0 / jnp.sum(e, axis=1, keepdims=True))).astype(jnp.bfloat16)
            o = jnp.dot(p, v_ref[mb], preferred_element_type=jnp.float32).astype(jnp.bfloat16)
            o = o.reshape(CHIPS, CORES, rows, V_DIM)
            for d in range(CHIPS):
                outs[d][:, mb, :, hh * V_DIM:(hh + 1) * V_DIM] = o[d]


def attention(first_pair, cq_all, kv_all, w_qup, w_kvup, cos_q, sin_q, q_lo, q_hi, k_code, steps):
    rows = kv_all.shape[2]
    keys = kv_all.shape[0] * rows
    hw = HEADS_PER_STEP
    full = lambda a: pl.BlockSpec(a.shape, lambda i, s, n=a.ndim: (0,) * n)
    out = jax.ShapeDtypeStruct((CORES, MICRO, rows, steps * hw * V_DIM), jnp.bfloat16)
    flops = 2 * steps * hw * (MEMBERS * MICRO * rows * cq_all.shape[-1] * QK_DIM + MICRO * keys * KV_LAT * KV_HEAD + 2 * MICRO * MEMBERS * rows * keys * 256)
    return pl.pallas_call(
        attention_kernel,
        grid_spec=pltpu.PrefetchScalarGridSpec(
            num_scalar_prefetch=1,
            grid=(steps,),
            in_specs=[
                full(cq_all),
                full(kv_all),
                pl.BlockSpec((w_qup.shape[0], hw * QK_DIM), lambda i, s: (0, s[0] + i)),
                pl.BlockSpec((w_kvup.shape[0], hw * KV_HEAD), lambda i, s: (0, s[0] + i)),
                full(cos_q),
                full(sin_q),
                full(q_lo),
                full(q_hi),
                full(k_code),
            ],
            out_specs=[pl.BlockSpec((CORES, MICRO, rows, hw * V_DIM), lambda i, s: (0, 0, 0, i))] * CHIPS,
            scratch_shapes=[
                pltpu.VMEM((MICRO, keys, NOPE_DIM + LANES), jnp.bfloat16),
                pltpu.VMEM((MICRO, keys, V_DIM), jnp.bfloat16),
                pltpu.VMEM((MICRO, MEMBERS * rows, keys), jnp.float32),
            ],
        ),
        out_shape=[out] * CHIPS,
        compiler_params=pltpu.CompilerParams(dimension_semantics=("arbitrary",), vmem_limit_bytes=VMEM_LIMIT),
        cost_estimate=pl.CostEstimate(flops=flops, bytes_accessed=steps * hw * 2 * (1536 * 192 + 512 * 256), transcendentals=0),
        name="attention",
    )(first_pair, cq_all, kv_all, w_qup, w_kvup, cos_q, sin_q, q_lo, q_hi, k_code)


def out_kernel(k_blocks, per_piece, *refs):
    piece_refs = refs[:CHIPS]
    w_ref = refs[CHIPS]
    acc_in = refs[CHIPS + 1:-1] if len(refs) > CHIPS + 2 else ()
    y_ref = refs[-1]
    i = pl.program_id(0)
    rows = y_ref.shape[0]
    blk = w_ref.shape[0]

    def product(d):
        return jnp.dot(piece_refs[d][...].reshape(rows, blk), w_ref[...], preferred_element_type=jnp.float32)

    for d in range(CHIPS):
        @pl.when(i // per_piece == d)
        def _(d=d):
            if d == 0:
                @pl.when(i == 0)
                def _():
                    base = product(0)
                    y_ref[...] = base + acc_in[0][...] if acc_in else base
                @pl.when(i > 0)
                def _():
                    y_ref[...] += product(0)
            else:
                y_ref[...] += product(d)


def out_project(w_rows, pieces, w_out, acc):
    rows = CORES * MICRO * pieces[0].shape[2]
    depth = pieces[0].shape[3]
    blk = 512
    per_piece = depth // blk
    steps = CHIPS * per_piece
    cols = w_out.shape[1]

    def kern(s, *refs):
        return out_kernel(steps, per_piece, *refs)

    piece_specs = [
        pl.BlockSpec(pieces[0].shape[:3] + (blk,), lambda i, s, d=d: (0, 0, 0, jnp.clip(i - d * per_piece, 0, per_piece - 1)))
        for d in range(CHIPS)
    ]
    extra = [] if acc is None else [acc]
    return pl.pallas_call(
        kern,
        grid_spec=pltpu.PrefetchScalarGridSpec(
            num_scalar_prefetch=1,
            grid=(steps,),
            in_specs=piece_specs
            + [pl.BlockSpec((blk, cols), lambda i, s: (s[i // per_piece] + i % per_piece, 0))]
            + [pl.BlockSpec((rows, cols), lambda i, s: (0, 0))] * len(extra),
            out_specs=pl.BlockSpec((rows, cols), lambda i, s: (0, 0)),
        ),
        out_shape=jax.ShapeDtypeStruct((rows, cols), jnp.float32),
        compiler_params=pltpu.CompilerParams(dimension_semantics=("arbitrary",), vmem_limit_bytes=VMEM_LIMIT),
        cost_estimate=pl.CostEstimate(flops=2 * rows * CHIPS * depth * cols, bytes_accessed=2 * CHIPS * depth * cols, transcendentals=0),
        name="out_project",
    )(w_rows, *pieces, w_out, *extra)


def solution(mesh):
    tok_spec = P(("dp", "sp"), None)
    idx_spec = P(("dp", "sp"))
    group = mesh.shape["sp"]

    def flip_perm(mask):
        return [(i, i ^ mask) for i in range(group)]

    def local_body(x_one, seg_one, pos_one, x_two, seg_two, pos_two, w_qdown, gain_q, w_qup, w_kvdown, gain_kv, w_kvup, w_out):
        rows = x_one.shape[0]
        heads = w_out.shape[0] // V_DIM
        my_heads = heads // MEMBERS
        me = lax.axis_index("sp")
        core = me % CORES
        chip_in_square = (me // X_BIT) % 2 + 2 * ((me // Y_BIT) % 2)

        x_both = jnp.concatenate([x_one, x_two], axis=0)
        pos = jnp.concatenate([pos_one, pos_two])
        seg = jnp.concatenate([seg_one, seg_two])
        kv_raw = jnp.dot(x_both, w_kvdown, preferred_element_type=jnp.float32)
        kv_latent = rms_scale(kv_raw[:, :KV_LAT], gain_kv)
        cos_k, sin_k = rope_tables(pos)
        k_rope = rope_rotate(kv_raw[:, KV_LAT:], cos_k, sin_k).astype(jnp.bfloat16)
        q_latent = rms_scale(jnp.dot(x_both, w_qdown, preferred_element_type=jnp.float32), gain_q)
        meta = jnp.stack([seg, pos // 32, pos % 32], axis=1).astype(jnp.bfloat16)
        meta = jnp.pad(meta, ((0, 0), (0, LANES - ROPE_DIM - 3)))
        packed = jnp.concatenate([kv_latent, k_rope, meta], axis=1).reshape(MICRO, rows, KV_PACK)
        cq_all, kv_all = gather_latents(q_latent.reshape(MICRO, rows, -1), packed, group)

        tags = kv_all[..., KV_LAT + ROPE_DIM:KV_LAT + ROPE_DIM + 3].astype(jnp.int32)
        seg_all = tags[..., 0]
        pos_all = tags[..., 1] * 32 + tags[..., 2]
        limit = group * rows
        code = seg_all * limit + pos_all
        k_code = code.transpose(1, 0, 2).reshape(MICRO, 1, group * rows)
        members = jnp.stack([jnp.bitwise_xor(me, mask + c) for mask in CHIP_MASKS for c in range(CORES)])
        q_pos = pos_all[members]
        q_hi = code[members].transpose(1, 0, 2).reshape(MICRO, MEMBERS * rows, 1)
        q_lo = q_hi - q_pos.transpose(1, 0, 2).reshape(MICRO, MEMBERS * rows, 1)
        cos_q, sin_q = rope_tables(q_pos.reshape(-1))
        cos_q = jnp.concatenate([cos_q, cos_q], axis=1)
        sin_q = jnp.concatenate([-sin_q, sin_q], axis=1)

        head0 = core * (heads // CORES) + chip_in_square * my_heads
        chunk_heads = my_heads // CHUNKS
        steps = chunk_heads // HEADS_PER_STEP
        blk = 512
        acc = None
        all_pieces = []
        for j in range(CHUNKS):
            first_pair = ((head0 + j * chunk_heads) // HEADS_PER_STEP).astype(jnp.int32).reshape(1)
            outs = attention(first_pair, cq_all, kv_all, w_qup, w_kvup, cos_q, sin_q, q_lo, q_hi, k_code, steps)
            pieces = [outs[0]] + [lax.ppermute(outs[d], "sp", flip_perm(CHIP_MASKS[d])) for d in range(1, CHIPS)]
            all_pieces.append(pieces)
        for j in range(CHUNKS):
            owners = [core * (heads // CORES) + jnp.bitwise_xor(chip_in_square, d) * my_heads + j * chunk_heads for d in range(CHIPS)]
            w_rows = (jnp.stack(owners) * V_DIM // blk).astype(jnp.int32)
            acc = out_project(w_rows, all_pieces[j], w_out, acc)
        y_rows = MICRO * rows
        other = lax.ppermute(acc[y_rows:], "sp", flip_perm(1))
        y = (acc[:y_rows] + other).astype(jnp.bfloat16)
        return y[:rows], y[rows:]

    rep = P()
    return jax.shard_map(
        local_body,
        mesh=mesh,
        in_specs=(tok_spec, idx_spec, idx_spec, tok_spec, idx_spec, idx_spec, rep, rep, rep, rep, rep, rep, rep),
        out_specs=(tok_spec, tok_spec),
        check_vma=False,
    )
```

time: 421 us -> 168 us (0.40); the launches traced: 414 us -> 168 us
  matrix products: 217 us -> 12.9 us
  Pallas kernels: 0 us -> 124 us
  blocking collectives: 111 us -> 0 us
  other arithmetic: 30.8 us -> 8.91 us
  between operations: 14.5 us -> 1.06 us
  waiting for transfers between devices: 15.5 us -> 2.68 us
  starting transfers between devices: 17.4 us -> 7.31 us
    dot_general x16 -> x2, matrix products: 217 us -> 12.9 us  [the longest x1 8.38 us: local_body(): jnp.dot(x_both, w_qdown, preferred_element_type=jnp.float32)]
    pallas_call x0 -> x5, Pallas kernels: none -> 124 us  [the longest x2 49.5 us: attention(): pl.pallas_call(attention_kernel, grid_spec=pltpu.PrefetchScalarGridSpec(n...]
    all_gather x2 -> x0, blocking collectives: 61.2 us -> none  [micro_block(): rope_all = lax.all_gather(k_rope, 'sp', axis=0, tiled=True)]
    unnamed x1 -> x0, blocking collectives: 50.1 us -> none
    sub x2 -> x1, other arithmetic: 24.1 us -> 0.01 us  [local_body(): q_lo = q_hi - q_pos.transpose(1, 0, 2).reshape(MICRO, MEMBERS * rows, 1)]
    all_to_all x2 -> x0, starting transfers between devices: 17.1 us -> none  [micro_block(): tok_out = lax.all_to_all(head_out, 'sp', 0, 1, tiled=True)]
    all_to_all x2 -> x0, waiting for transfers between devices: 14.1 us -> none  [micro_block(): tok_out = lax.all_to_all(head_out, 'sp', 0, 1, tiled=True)]
    ppermute x0 -> x7, starting transfers between devices: none -> 7.31 us  [the longest x6 5.43 us: local_body(): lax.ppermute(outs[d], 'sp', flip_perm(CHIP_MASKS[d]))]
  transfers between devices with their start and end apart: 6 -> 7, of which waited for: 1 -> 1; matrix products, arithmetic and copies ran while one was open for 33% -> 1% of each run, Pallas kernels for 0% -> 26%
where the time goes in v1:
time: 168 us
  Pallas kernels  124 us (74%)
  matrix products  12.9 us (8%)
  local copies, waits for them, and re-layouts  11.3 us (7%)
  other arithmetic  8.91 us (5%)
  starting transfers between devices  7.31 us (4%)
  waiting for transfers between devices  2.68 us (2%)
    pallas_call x2, Pallas kernels, attention(): pl.pallas_call(attention_kernel, grid_spec=pltpu.PrefetchScalarGridSpec(n...  49.5 us
    pallas_call x2, Pallas kernels, out_project(): pl.pallas_call(kern, grid_spec=pltpu.PrefetchScalarGridSpec(num_scalar_pr...  38 us
    pallas_call x1, Pallas kernels, gather_latents(): pl.pallas_call(gather_kernel, out_shape=(jax.ShapeDtypeStruct((CHIPS, COR...  36.2 us
    dot_general x1, matrix products, local_body(): jnp.dot(x_both, w_qdown, preferred_element_type=jnp.float32)  8.38 us
    ppermute x6, starting transfers between devices, local_body(): lax.ppermute(outs[d], 'sp', flip_perm(CHIP_MASKS[d]))  5.43 us
    dot_general x1, matrix products, local_body(): kv_raw = jnp.dot(x_both, w_kvdown, preferred_element_type=jnp.float32)  4.53 us
  transfers between devices with their start and end apart: 7, of which 1 were waited for; matrix products, arithmetic and copies ran while one was open for 1% of the time, Pallas kernels for 26%

profile of v1, /device:TPU:97, one launch (start us, length us, event | category | flops | bytes accessed | tf_op | source)
XLA Modules:
  0.0 167.8 jit_solution(6578446962614836053)
XLA Ops:
  0.7 1.0 constant_dynamic-update-slice_fusion.1
  1.7 1.0 constant_dynamic-update-slice_fusion
  2.7 4.5 %fusion.17 = f32[64,576]{1,0:T(8,128)S(1)} fusion(bf16[64,5120]{1,0:T(8,128)(2,1)S(1)} %constant_dynamic-update-slice_fusion, bf16[5120,576]{0,1:T(8,128)(2,1)} %param.22), kind=kOutput, calls=%fused_computation.62 | convolution fusion | flops 377487360 | bytes 6701056 | tf_op jit(solution)/shard_map/dot_general | solution.py:366
  7.5 8.4 %multiply_reduce_fusion = (f32[64]{0:T(128)S(1)}, f32[64,1536]{1,0:T(8,128)S(1)}) fusion(bf16[64,5120]{1,0:T(8,128)(2,1)S(1)} %constant_dynamic-update-slice_fusion, bf16[5120,1536]{1,0:T(8,128)(2,1)} %param.19), kind=kOutput, calls=%fused_computation.9 | convolution fusion | flops 1006829504 | bytes 16777472 | tf_op jit(solution)/shard_map/dot_general | solution.py:370
  17.0 0.8 multiply_convert_fusion
  17.8 0.7 fusion.3
  18.5 36.2 %gather_latents.1 = (bf16[4,2,2,32,1536]{4,3,2,1,0:T(8,128)(2,1)}, bf16[32,2,32,640]{3,2,1,0:T(8,128)(2,1)}) custom-call(bf16[2,32,1536]{2,1,0:T(8,128)(2,1)} %bitcast.37, bf16[2,32,640]{2,1,0:T(8,128)(2,1)} %bitcast.38), custom_call_target="tpu_custom_call" | custom-call | tf_op jit(solution)/shard_map/gather_latents/pallas_call | solution.py:186
  54.7 1.3 slice_convert_fusion
  58.0 1.0 fusion.2
  60.2 0.9 copy.87.qhi_ref
  61.1 0.9 copy.86.qlo_ref
  62.6 1.0 pad_maximum_fusion
  63.6 24.8 %attention.3 = (bf16[2,2,32,1024]{3,2,1,0:T(8,128)(2,1)}, bf16[2,2,32,1024]{3,2,1,0:T(8,128)(2,1)}, bf16[2,2,32,1024]{3,2,1,0:T(8,128)(2,1)}, bf16[2,2,32,1024]{3,2,1,0:T(8,128)(2,1)}) custom-call(s32[1]{0:T(128)} %bitcast.28.first_pair, bf16[4,2,2,32,1536]{4,3,2,1,0:T(8,128)(2,1)} %get-tuple-element.12.cq_ref, ...), custom_call_target="tpu_custom_call" | custom-call | flops 11005853696 | bytes 6815744 | tf_op jit(solution)/shard_map/attention/pallas_call | solution.py:257
  88.6 2.5 %collective-permute-start.5 = (bf16[2,2,32,1024]{3,2,1,0:T(8,128)(2,1)}, bf16[2,2,32,1024]{3,2,1,0:T(8,128)(2,1)S(1)}, u32[]{:S(2)}, u32[]{:S(2)}) collective-permute-start(bf16[2,2,32,1024]{3,2,1,0:T(8,128)(2,1)} %get-tuple-element.21), channel_id=1, source_target_pairs={{0,10},{1,11},{2,8},{3,9},{4,14},{5,15},{6,12},{7,13},{8,2},{9,3},... | collective-permute-start | bytes 786440 | tf_op jit(solution)/shard_map/ppermute | solution.py:399
  91.1 24.7 %attention.2 = (bf16[2,2,32,1024]{3,2,1,0:T(8,128)(2,1)}, bf16[2,2,32,1024]{3,2,1,0:T(8,128)(2,1)}, bf16[2,2,32,1024]{3,2,1,0:T(8,128)(2,1)}, bf16[2,2,32,1024]{3,2,1,0:T(8,128)(2,1)}) custom-call(s32[1]{0:T(128)} %bitcast.4.first_pair, bf16[4,2,2,32,1536]{4,3,2,1,0:T(8,128)(2,1)} %get-tuple-element.12.cq_ref, ...), custom_call_target="tpu_custom_call" | custom-call | flops 11005853696 | bytes 6815744 | tf_op jit(solution)/shard_map/attention/pallas_call | solution.py:257
  117.7 2.1 %collective-permute-start.2 = (bf16[2,2,32,1024]{3,2,1,0:T(8,128)(2,1)}, bf16[2,2,32,1024]{3,2,1,0:T(8,128)(2,1)S(1)}, u32[]{:S(2)}, u32[]{:S(2)}) collective-permute-start(bf16[2,2,32,1024]{3,2,1,0:T(8,128)(2,1)} %get-tuple-element.17), channel_id=1, source_target_pairs={{0,10},{1,11},{2,8},{3,9},{4,14},{5,15},{6,12},{7,13},{8,2},{9,3},... | collective-permute-start | bytes 786440 | tf_op jit(solution)/shard_map/ppermute | solution.py:399
  119.9 0.7 copy-done.1
  120.6 18.5 %out_project.2.refs_5_ = f32[128,5120]{1,0:T(8,128)} custom-call(s32[4]{0:T(128)} %and_select_fusion.s, bf16[2,2,32,1024]{3,2,1,0:T(8,128)(2,1)} %get-tuple-element.18.refs_0_, bf16[2,2,32,1024]{3,2,1,0:T(8,128)(2,1)} %copy-done, bf16[2,2,32,1024]{3,2,1,0:T(8,128)(2,1)} %copy-done.1, bf16[2,2,32,1024]{3,2,1,0:T(8,128)(2,1)} %copy-done.2, ...), custom_call_target="tpu_custom_call" | custom-call | flops 5368709120 | bytes 41943040 | tf_op jit(solution)/shard_map/out_project/pallas_call | solution.py:330
  140.0 19.5 %out_project.3 = f32[128,5120]{1,0:T(8,128)} custom-call(s32[4]{0:T(128)} %and_select_fusion.3.s, bf16[2,2,32,1024]{3,2,1,0:T(8,128)(2,1)} %get-tuple-element.14.refs_0_, bf16[2,2,32,1024]{3,2,1,0:T(8,128)(2,1)} %copy-done.3, bf16[2,2,32,1024]{3,2,1,0:T(8,128)(2,1)} %copy-done.4, bf16[2,2,32,1024]{3,2,1,0:T(8,128)(2,1)} %copy-done.5, ...), custom_call_target="tpu_custom_call" | custom-call | flops 5368709120 | bytes 41943040 | tf_op jit(solution)/shard_map/out_project/pallas_call | solution.py:330
  159.5 1.4 slice.58
  160.9 1.9 %collective-permute-start.6 = (f32[64,5120]{1,0:T(8,128)S(1)}, f32[64,5120]{1,0:T(8,128)S(1)}, u32[]{:S(2)}, u32[]{:S(2)}) collective-permute-start(f32[64,5120]{1,0:T(8,128)S(1)} %slice.58), channel_id=1, source_target_pairs={{0,1},{1,0},{2,3},{3,2},{4,5},{5,4},{6,7},{7,6},{8,9},{9,8},{10,11... | collective-permute-start | bytes 3932168 | tf_op jit(solution)/shard_map/ppermute | solution.py:406
  162.8 2.7 %collective-permute-done.6 = f32[64,5120]{1,0:T(8,128)S(1)} collective-permute-done((f32[64,5120]{1,0:T(8,128)S(1)}, f32[64,5120]{1,0:T(8,128)S(1)}, u32[]{:S(2)}, u32[]{:S(2)}) %collective-permute-start.6) | collective-permute-done | bytes 1310752 | tf_op jit(solution)/shard_map/ppermute | solution.py:406
  165.5 1.5 fusion
  167.0 0.9 fusion.15
  (75 shorter events, 8.0 us)
Async XLA Ops:
  7.5 8.5 %copy-start.6 = (bf16[1536]{0:T(1024)(128)(2,1)S(1)}, bf16[1536]{0:T(1024)(128)(2,1)}, u32[]{:S(2)}) copy-start(bf16[1536]{0:T(1024)(128)(2,1)} %param.20) | copy-start | bytes 9220
  7.5 8.5 %copy-start.8 = (s32[32]{0:T(128)S(1)}, s32[32]{0:T(128)}, u32[]{:S(2)}) copy-start(s32[32]{0:T(128)} %param.18) | copy-start | bytes 388
  7.5 8.5 %copy-start.9 = (s32[32]{0:T(128)S(1)}, s32[32]{0:T(128)}, u32[]{:S(2)}) copy-start(s32[32]{0:T(128)} %param.15) | copy-start | bytes 388
  7.5 8.6 %copy-start.10 = (s32[32]{0:T(128)S(1)}, s32[32]{0:T(128)}, u32[]{:S(2)}) copy-start(s32[32]{0:T(128)} %param.17) | copy-start | bytes 388
  7.5 8.6 %copy-start.11 = (s32[32]{0:T(128)S(1)}, s32[32]{0:T(128)}, u32[]{:S(2)}) copy-start(s32[32]{0:T(128)} %param.14) | copy-start | bytes 388
  7.5 9.4 %copy-start.7 = (bf16[512]{0:T(512)(128)(2,1)S(1)}, bf16[512]{0:T(512)(128)(2,1)}, u32[]{:S(2)}) copy-start(bf16[512]{0:T(512)(128)(2,1)} %param.23) | copy-start | bytes 3076
  88.4 29.3 %collective-permute-start.3 = (bf16[2,2,32,1024]{3,2,1,0:T(8,128)(2,1)}, bf16[2,2,32,1024]{3,2,1,0:T(8,128)(2,1)S(1)}, u32[]{:S(2)}, u32[]{:S(2)}) collective-permute-start(bf16[2,2,32,1024]{3,2,1,0:T(8,128)(2,1)} %get-tuple-element.19), channel_id=1, source_target_pairs={{0,2},{1,3},{2,0},{3,1},{4,6},{5,7},{6,4},{7,5},{8,10},{9,11},{10,... | collective-permute-start | bytes 786440 | tf_op jit(solution)/shard_map/ppermute | solution.py:399
  88.5 31.4 %collective-permute-start.4 = (bf16[2,2,32,1024]{3,2,1,0:T(8,128)(2,1)}, bf16[2,2,32,1024]{3,2,1,0:T(8,128)(2,1)S(1)}, u32[]{:S(2)}, u32[]{:S(2)}) collective-permute-start(bf16[2,2,32,1024]{3,2,1,0:T(8,128)(2,1)} %get-tuple-element.20), channel_id=1, source_target_pairs={{0,8},{1,9},{2,10},{3,11},{4,12},{5,13},{6,14},{7,15},{8,0},{9,1},... | collective-permute-start | bytes 786440 | tf_op jit(solution)/shard_map/ppermute | solution.py:399
  88.6 31.3 %collective-permute-start.5 = (bf16[2,2,32,1024]{3,2,1,0:T(8,128)(2,1)}, bf16[2,2,32,1024]{3,2,1,0:T(8,128)(2,1)S(1)}, u32[]{:S(2)}, u32[]{:S(2)}) collective-permute-start(bf16[2,2,32,1024]{3,2,1,0:T(8,128)(2,1)} %get-tuple-element.21), channel_id=1, source_target_pairs={{0,10},{1,11},{2,8},{3,9},{4,14},{5,15},{6,12},{7,13},{8,2},{9,3},... | collective-permute-start | bytes 786440 | tf_op jit(solution)/shard_map/ppermute | solution.py:399
  115.8 23.3 %collective-permute-start = (bf16[2,2,32,1024]{3,2,1,0:T(8,128)(2,1)}, bf16[2,2,32,1024]{3,2,1,0:T(8,128)(2,1)S(1)}, u32[]{:S(2)}, u32[]{:S(2)}) collective-permute-start(bf16[2,2,32,1024]{3,2,1,0:T(8,128)(2,1)} %get-tuple-element.15), channel_id=1, source_target_pairs={{0,2},{1,3},{2,0},{3,1},{4,6},{5,7},{6,4},{7,5},{8,10},{9,11},{10,... | collective-permute-start | bytes 786440 | tf_op jit(solution)/shard_map/ppermute | solution.py:399
  116.0 23.1 %collective-permute-start.1 = (bf16[2,2,32,1024]{3,2,1,0:T(8,128)(2,1)}, bf16[2,2,32,1024]{3,2,1,0:T(8,128)(2,1)S(1)}, u32[]{:S(2)}, u32[]{:S(2)}) collective-permute-start(bf16[2,2,32,1024]{3,2,1,0:T(8,128)(2,1)} %get-tuple-element.16), channel_id=1, source_target_pairs={{0,8},{1,9},{2,10},{3,11},{4,12},{5,13},{6,14},{7,15},{8,0},{9,1},... | collective-permute-start | bytes 786440 | tf_op jit(solution)/shard_map/ppermute | solution.py:399
  117.7 2.2 %copy-start = (bf16[2,2,32,1024]{3,2,1,0:T(8,128)(2,1)}, bf16[2,2,32,1024]{3,2,1,0:T(8,128)(2,1)S(1)}, u32[]{:S(2)}) copy-start(bf16[2,2,32,1024]{3,2,1,0:T(8,128)(2,1)S(1)} %collective-permute-done.3.refs_1_) | copy-start | bytes 786436
  117.7 21.4 %collective-permute-start.2 = (bf16[2,2,32,1024]{3,2,1,0:T(8,128)(2,1)}, bf16[2,2,32,1024]{3,2,1,0:T(8,128)(2,1)S(1)}, u32[]{:S(2)}, u32[]{:S(2)}) collective-permute-start(bf16[2,2,32,1024]{3,2,1,0:T(8,128)(2,1)} %get-tuple-element.17), channel_id=1, source_target_pairs={{0,10},{1,11},{2,8},{3,9},{4,14},{5,15},{6,12},{7,13},{8,2},{9,3},... | collective-permute-start | bytes 786440 | tf_op jit(solution)/shard_map/ppermute | solution.py:399
  119.8 0.7 copy-start.1
  119.8 0.8 copy-start.2
  139.1 0.7 copy-start.3
  139.1 0.8 copy-start.4
  139.1 0.8 copy-start.5
  160.9 4.5 %collective-permute-start.6 = (f32[64,5120]{1,0:T(8,128)S(1)}, f32[64,5120]{1,0:T(8,128)S(1)}, u32[]{:S(2)}, u32[]{:S(2)}) collective-permute-start(f32[64,5120]{1,0:T(8,128)S(1)} %slice.58), channel_id=1, source_target_pairs={{0,1},{1,0},{2,3},{3,2},{4,5},{5,4},{6,7},{7,6},{8,9},{9,8},{10,11... | collective-permute-start | bytes 3932168 | tf_op jit(solution)/shard_map/ppermute | solution.py:406

commit v2 on v0

v2 whole, which is shorter than its diff:
```python
import functools

import jax
import jax.numpy as jnp
from jax import lax
from jax.experimental import pallas as pl
from jax.experimental.pallas import tpu as pltpu
from jax.sharding import PartitionSpec as P

NOPE_DIM = 128
ROPE_DIM = 64
KV_LAT = 512
V_DIM = 128
QK_DIM = NOPE_DIM + ROPE_DIM
KV_HEAD = NOPE_DIM + V_DIM
ROPE_BASE = 10000.0
NORM_EPS = 1e-6
LANES = 128

CORES = 2
ROW = 4
CHIPS = 4
MEMBERS = CHIPS * CORES
MICRO = 2
KV_PACK = KV_LAT + LANES
HEADS_PER_STEP = 2
SOFT_ROWS = 16
OUT_COLS = 256
OUT_SLOTS = 7
LAG = 3
VMEM_LIMIT = 67_043_328
MESH = pl.DeviceIdType.MESH


def rms_scale(pre_norm, gain_vec):
    mean_sq = jnp.mean(pre_norm * pre_norm, axis=-1, keepdims=True)
    return (pre_norm * lax.rsqrt(mean_sq + NORM_EPS) * gain_vec.astype(jnp.float32)).astype(jnp.bfloat16)


def rope_tables(positions):
    half_dim = ROPE_DIM // 2
    inv_freq = ROPE_BASE ** (-jnp.arange(half_dim, dtype=jnp.float32) / half_dim)
    angles = positions.astype(jnp.float32)[..., None] * inv_freq
    return jnp.cos(angles), jnp.sin(angles)


def rope_rotate(rot_in, cos_tab, sin_tab):
    half_dim = ROPE_DIM // 2
    first_half = rot_in[..., :half_dim]
    second_half = rot_in[..., half_dim:]
    return jnp.concatenate([first_half * cos_tab - second_half * sin_tab, second_half * cos_tab + first_half * sin_tab], axis=-1)


def place():
    me = lax.axis_index("sp")
    core = me % CORES
    chip = me // CORES
    x = chip % ROW
    y = chip // ROW

    def dev(dy, dx):
        return (((y + dy + ROW) % ROW) * ROW + (x + dx + ROW) % ROW) * CORES + core

    def near(first, second):
        return dev(core * first + (1 - core) * second, (1 - core) * first + core * second)

    flip_x = 1 - 2 * (x % 2)
    flip_y = 1 - 2 * (y % 2)
    square = (me, dev(0, flip_x), dev(flip_y, 0), dev(flip_y, flip_x))
    corner = tuple((d % 2) * (1 - x % 2) + (1 - d % 2) * (x % 2) + 2 * ((d // 2) * (1 - y % 2) + (1 - d // 2) * (y % 2)) for d in range(CHIPS))
    return me, core, me + 1 - 2 * core, square, corner, near


def meet(peers):
    barrier = pltpu.get_barrier_semaphore()
    for peer in peers:
        pl.semaphore_signal(barrier, inc=1, device_id={"sp": peer}, device_id_type=MESH)
    pl.semaphore_wait(barrier, len(peers))


def gather(where, cq_ref, kv_ref, tab_ref, cq_all, kv_all, tab_all, loc, send_sems, recv_sems):
    me, _, sib, square, _, near = where
    right1, left1, right2, left2 = near(1, 0), near(-1, 0), near(0, 1), near(0, -1)
    copies = []

    def send(src, dst, to):
        n = len(copies)
        copy = pltpu.make_async_remote_copy(
            src_ref=src, dst_ref=dst, send_sem=send_sems.at[n], recv_sem=recv_sems.at[n], device_id={"sp": to}, device_id_type=MESH
        )
        copy.start()
        copies.append(copy)
        return copy

    handed = []

    def send_kv(owner, to, part=None):
        at = (owner,) if part is None else (owner, part)
        return send(kv_all.at[at], kv_all.at[at], to)

    def hand_kv(owner):
        handed.append(send_kv(owner, sib))

    def hand(slot):
        handed.append(send(cq_all.at[slot, 0], cq_all.at[slot, 1], sib))
        handed.append(send(tab_all.at[slot, 0], tab_all.at[slot, 1], sib))

    own = (
        pltpu.make_async_copy(kv_ref, kv_all.at[me], loc.at[0]),
        pltpu.make_async_copy(cq_ref, cq_all.at[0, 0], loc.at[1]),
        pltpu.make_async_copy(tab_ref, tab_all.at[0, 0], loc.at[2]),
    )
    for copy in own:
        copy.start()
    first_r = send(kv_ref, kv_all.at[me], right1)
    first_l = send(kv_ref, kv_all.at[me], left1)
    second = {0: (send(kv_ref, kv_all.at[me], right2), send(kv_ref, kv_all.at[me], left2))}
    tab_in = {s: send(tab_ref, tab_all.at[s, 0], square[s]) for s in (1, 2, 3)}
    cq_in = {s: send(cq_ref, cq_all.at[s, 0], square[s]) for s in (1, 2)}
    handed.append(send(kv_ref, kv_all.at[me], sib))
    handed.append(send(cq_ref, cq_all.at[0, 1], sib))
    handed.append(send(tab_ref, tab_all.at[0, 1], sib))

    first_r.wait_recv()
    far_r = send_kv(left1, right1, 0)
    second[-1] = (send_kv(left1, right2), send_kv(left1, left2))
    hand_kv(left1)
    first_l.wait_recv()
    far_l = send_kv(right1, left1, 1)
    second[1] = (send_kv(right1, right2), send_kv(right1, left2))
    hand_kv(right1)

    def pass_on(first):
        r, l = second[first]
        below, above = near(first, -1), near(first, 1)
        r.wait_recv()
        up = send_kv(below, right2, 0)
        hand_kv(below)
        l.wait_recv()
        down = send_kv(above, left2, 1)
        hand_kv(above)
        return up, down

    last = {0: pass_on(0)}
    far = near(2, 0)
    far_r.wait_recv()
    far_l.wait_recv()
    second[2] = (send_kv(far, right2), send_kv(far, left2))
    hand_kv(far)

    cq_in[1].wait_recv()
    tab_in[1].wait_recv()
    diag_a = send(cq_all.at[1, 0, 0], cq_all.at[3, 0, 0], square[2])
    hand(1)
    cq_in[2].wait_recv()
    tab_in[2].wait_recv()
    diag_b = send(cq_all.at[2, 0, 1], cq_all.at[3, 0, 1], square[1])
    hand(2)

    for first in (-1, 1, 2):
        last[first] = pass_on(first)
    diag_a.wait_recv()
    diag_b.wait_recv()
    tab_in[3].wait_recv()
    hand(3)
    for first in (0, -1, 1, 2):
        for copy in last[first]:
            copy.wait_recv()
        hand_kv(near(first, 2))
    for copy in handed:
        copy.wait_recv()
    for copy in copies:
        copy.wait_send()
    for copy in own:
        copy.wait()


N_COPIES = 4 + 3 + 2 + 3 + 2 + 4 * 2 + 2 * 3 + 15 + 2 + 6


def block_kernel(
    cq_ref, kv_ref0, tab_ref0, wqup_ref, wkvup_ref, wout_ref, y1_ref, y2_ref,
    cq_ref_all, kv_ref, tab_ref, wq_buf, wkv_buf, wo_buf, o_ref, o_in, y_own, y_far, y_in,
    kcat_ref, v_ref, qcat_ref, s_ref, p_ref, mask_ref,
    loc, g_send, g_recv, w_sem, wo_sem, o_send_sem, o_recv_sem, y_send_sem, y_recv_sem,
):
    where = place()
    me, core, sib, square, corner, near = where
    devs, _, rows, _ = kv_ref.shape
    keys = devs * rows
    q_lat = cq_ref_all.shape[-1]
    chip_rows = CORES * rows
    q_rows = CHIPS * chip_rows
    key_devs = devs // 8
    key_chunk = key_devs * rows
    soft_rows = SOFT_ROWS
    steps = o_ref.shape[1]
    heads = wqup_ref.shape[1] // QK_DIM
    my_heads = heads // MEMBERS
    n_blocks, _, blk = y_in.shape
    slots = wo_buf.shape[0]
    to_exp2 = QK_DIM ** -0.5 * 1.4426950408889634

    def first_head(d):
        return core * (heads // CORES) + corner[d] * my_heads

    def weight_copies(i):
        slot = i % 2
        h = first_head(0) + HEADS_PER_STEP * i
        wq, wkv = HEADS_PER_STEP * QK_DIM, HEADS_PER_STEP * KV_HEAD
        return (
            pltpu.make_async_copy(wqup_ref.at[:, pl.ds(pl.multiple_of(h * QK_DIM, LANES), wq)], wq_buf.at[slot], w_sem.at[slot, 0]),
            pltpu.make_async_copy(wkvup_ref.at[:, pl.ds(pl.multiple_of(h * KV_HEAD, LANES), wkv)], wkv_buf.at[slot], w_sem.at[slot, 1]),
        )

    def out_copies(b):
        slot = b % slots
        depth = my_heads * V_DIM
        return [
            pltpu.make_async_copy(
                wout_ref.at[pl.ds(pl.multiple_of(first_head(d) * V_DIM, depth), depth), pl.ds(pl.multiple_of(b * blk, LANES), blk)],
                wo_buf.at[slot, d],
                wo_sem.at[slot, d],
            )
            for d in range(CHIPS)
        ]

    for copy in weight_copies(0):
        copy.start()

    @pl.loop(0, slots)
    def _(b):
        for copy in out_copies(b):
            copy.start()

    meet((sib, square[3], near(1, 0), near(-1, 0), near(0, 1), near(0, -1)))
    gather(where, cq_ref, kv_ref0, tab_ref0, cq_ref_all, kv_ref, tab_ref, loc, g_send, g_recv)

    lane = lax.broadcasted_iota(jnp.int32, (LANES, LANES), 1)
    weight = jnp.where(lane == ROPE_DIM, float(keys), jnp.where(lane == ROPE_DIM + 1, 32.0, jnp.where(lane == ROPE_DIM + 2, 1.0, 0.0)))
    weight_pos = jnp.where(lane == ROPE_DIM, 0.0, weight)
    nt = (((1,), (1,)), ((), ()))
    for mb in range(MICRO):
        tail = kv_ref[:, mb, :, KV_LAT:].reshape(keys, LANES)
        for par in range(HEADS_PER_STEP):
            kcat_ref[par, mb, :, NOPE_DIM:] = tail
        k_code = lax.dot_general(weight.astype(jnp.bfloat16), tail, nt, preferred_element_type=jnp.float32)
        for r in range(MEMBERS):
            owner = square[r // CORES] + (r % CORES) * (1 - 2 * core)
            mine = kv_ref[owner, mb, :, KV_LAT:]
            q_code = lax.dot_general(mine, weight.astype(jnp.bfloat16), nt, preferred_element_type=jnp.float32)
            q_pos = lax.dot_general(mine, weight_pos.astype(jnp.bfloat16), nt, preferred_element_type=jnp.float32)
            hi = q_code[:, :1]
            lo = (q_code - q_pos)[:, :1]
            row = k_code[:1, :]
            mask_ref[mb, r * rows:(r + 1) * rows, :] = jnp.where((row >= lo) & (row <= hi), 1.0, 0.0)

    def kv_part(slot, par, c):
        latent = kv_ref[c * key_devs:(c + 1) * key_devs, :, :, :KV_LAT].reshape(key_devs * MICRO * rows, KV_LAT)
        kv = jnp.dot(latent, wkv_buf[slot, :, par * KV_HEAD:(par + 1) * KV_HEAD], preferred_element_type=jnp.float32)
        kv = kv.astype(jnp.bfloat16).reshape(key_devs, MICRO, rows, KV_HEAD)
        for mb in range(MICRO):
            one = kv[:, mb].reshape(key_chunk, KV_HEAD)
            kcat_ref[par, mb, c * key_chunk:(c + 1) * key_chunk, :NOPE_DIM] = one[:, :NOPE_DIM]
            v_ref[par, mb, c * key_chunk:(c + 1) * key_chunk, :] = one[:, NOPE_DIM:]

    def q_part(slot, par, d):
        cq = cq_ref_all[d].reshape(CORES * MICRO * rows, q_lat)
        f = jnp.dot(cq, wq_buf[slot, :, par * QK_DIM:(par + 1) * QK_DIM], preferred_element_type=jnp.float32)
        tab = tab_ref[d].reshape(CORES * MICRO * rows, 2 * ROPE_DIM)
        z = f[:, NOPE_DIM:]
        turned = jnp.concatenate([z[:, ROPE_DIM // 2:], z[:, :ROPE_DIM // 2]], axis=1)
        rot = z * tab[:, :ROPE_DIM] + turned * tab[:, ROPE_DIM:]
        pad = jnp.zeros((rot.shape[0], LANES - ROPE_DIM), jnp.float32)
        q = jnp.concatenate([f[:, :NOPE_DIM], rot, pad], axis=1).astype(jnp.bfloat16)
        q = q.reshape(CORES, MICRO, rows, NOPE_DIM + LANES)
        for mb in range(MICRO):
            qcat_ref[par, mb, d * chip_rows:(d + 1) * chip_rows, :] = q[:, mb].reshape(chip_rows, NOPE_DIM + LANES)

    def score_part(par, mb, n):
        cols = slice(n * 256, (n + 1) * 256)
        s_ref[par, mb, :, cols] = lax.dot_general(
            qcat_ref[par, mb], kcat_ref[par, mb, cols, :], (((1,), (1,)), ((), ())), preferred_element_type=jnp.float32
        )

    def soft_part(par, mb, r):
        at = slice(r * soft_rows, (r + 1) * soft_rows)
        s = jnp.where(mask_ref[mb, at, :] > 0.5, s_ref[par, mb, at, :], -1e30)
        e = jnp.exp2((s - jnp.max(s, axis=1, keepdims=True)) * to_exp2)
        p_ref[mb, at, :] = (e * (1.0 / jnp.sum(e, axis=1, keepdims=True))).astype(jnp.bfloat16)

    def value_part(par, mb, step):
        o = jnp.dot(p_ref[mb], v_ref[par, mb], preferred_element_type=jnp.float32).astype(jnp.bfloat16)
        o = o.reshape(CHIPS, CORES, rows, V_DIM)
        for d in range(CHIPS):
            o_ref[d, step, :, mb, :, par * V_DIM:(par + 1) * V_DIM] = o[d]

    def first_stage(slot, par):
        parts = [functools.partial(kv_part, slot, par, c) for c in range(8)]
        parts += [functools.partial(q_part, slot, par, d) for d in range(CHIPS)]
        parts += [functools.partial(score_part, par, mb, n) for mb in range(MICRO) for n in range(keys // 256)]
        return parts

    def second_stage(par, step):
        parts = []
        for mb in range(MICRO):
            parts += [functools.partial(soft_part, par, mb, r) for r in range(q_rows // soft_rows)]
            parts.append(functools.partial(value_part, par, mb, step))
        return parts

    def o_copies(step):
        return [
            pltpu.make_async_remote_copy(
                src_ref=o_ref.at[d, step],
                dst_ref=o_in.at[d - 1, step],
                send_sem=o_send_sem.at[d - 1, step],
                recv_sem=o_recv_sem.at[d - 1, step],
                device_id={"sp": square[d]},
                device_id_type=MESH,
            )
            for d in range(1, CHIPS)
        ]

    def beside(a, b):
        order = [((k + 0.5) / len(a), 0, f) for k, f in enumerate(a)] + [((k + 0.6) / len(b), 1, f) for k, f in enumerate(b)]
        for _, _, f in sorted(order, key=lambda v: v[:2]):
            f()

    @pl.loop(0, steps)
    def _(i):
        slot = i % 2
        before = jnp.maximum(i - 1, 0)
        for copy in weight_copies(i):
            copy.wait()

        @pl.when(i + 1 < steps)
        def _():
            for copy in weight_copies(i + 1):
                copy.start()

        beside(first_stage(slot, 0), second_stage(1, before))

        @pl.when(i > 0)
        def _():
            for copy in o_copies(before):
                copy.start()

        beside(first_stage(slot, 1), second_stage(0, i))

    for f in second_stage(1, steps - 1):
        f()
    for copy in o_copies(steps - 1):
        copy.start()

    @pl.loop(0, steps)
    def _(i):
        for copy in o_copies(i):
            copy.wait()

    def y_copy(b):
        return pltpu.make_async_remote_copy(
            src_ref=y_far.at[b], dst_ref=y_in.at[b], send_sem=y_send_sem.at[b], recv_sem=y_recv_sem.at[b], device_id={"sp": sib}, device_id_type=MESH
        )

    def finish(b):
        y_copy(b).wait()
        y = (y_own[b] + y_in[b]).astype(jnp.bfloat16)
        at = pl.ds(pl.multiple_of(b * blk, LANES), blk)
        y1_ref[:, at] = y[:rows]
        y2_ref[:, at] = y[rows:]

    @pl.loop(0, n_blocks)
    def _(b):
        slot = b % slots
        for copy in out_copies(b):
            copy.wait()
        total = None
        for d in range(CHIPS):
            src = o_ref.at[0] if d == 0 else o_in.at[d - 1]
            o = jnp.concatenate([src[s].reshape(CORES * MICRO * rows, HEADS_PER_STEP * V_DIM) for s in range(steps)], axis=1)
            term = jnp.dot(o, wo_buf[slot, d], preferred_element_type=jnp.float32)
            total = term if total is None else total + term
        y_own[b] = total[:MICRO * rows]
        y_far[b] = total[MICRO * rows:]
        y_copy(b).start()

        @pl.when(b + slots < n_blocks)
        def _():
            for copy in out_copies(b + slots):
                copy.start()

        @pl.when(b >= LAG)
        def _():
            finish(b - LAG)

    @pl.loop(n_blocks - LAG, n_blocks)
    def _(b):
        finish(b)


def latent_block(cq, kv, table, w_qup, w_kvup, w_out, group):
    rows = kv.shape[1]
    keys = group * rows
    q_rows = MEMBERS * rows
    hw = HEADS_PER_STEP
    heads = w_out.shape[0] // V_DIM
    steps = heads // MEMBERS // hw
    cols = w_out.shape[1]
    n_blocks = cols // OUT_COLS
    out = jax.ShapeDtypeStruct((rows, cols), jnp.bfloat16)
    dma = pltpu.SemaphoreType.DMA
    vmem, anywhere = pl.BlockSpec(memory_space=pltpu.VMEM), pl.BlockSpec(memory_space=pl.ANY)
    pair = (steps, CORES, MICRO, rows, hw * V_DIM)
    bf16, f32 = jnp.bfloat16, jnp.float32
    return pl.pallas_call(
        block_kernel,
        out_shape=(out, out),
        in_specs=[vmem] * 3 + [anywhere] * 3,
        out_specs=(vmem, vmem),
        scratch_shapes=[
            pltpu.VMEM((CHIPS, CORES) + cq.shape, bf16),
            pltpu.VMEM((group,) + kv.shape, bf16),
            pltpu.VMEM((CHIPS, CORES) + table.shape, f32),
            pltpu.VMEM((2, w_qup.shape[0], hw * QK_DIM), bf16),
            pltpu.VMEM((2, w_kvup.shape[0], hw * KV_HEAD), bf16),
            pltpu.VMEM((OUT_SLOTS, CHIPS, heads // MEMBERS * V_DIM, OUT_COLS), bf16),
            pltpu.VMEM((CHIPS,) + pair, bf16),
            pltpu.VMEM((CHIPS - 1,) + pair, bf16),
            pltpu.VMEM((n_blocks, MICRO * rows, OUT_COLS), f32),
            pltpu.VMEM((n_blocks, MICRO * rows, OUT_COLS), f32),
            pltpu.VMEM((n_blocks, MICRO * rows, OUT_COLS), f32),
            pltpu.VMEM((hw, MICRO, keys, NOPE_DIM + LANES), bf16),
            pltpu.VMEM((hw, MICRO, keys, V_DIM), bf16),
            pltpu.VMEM((hw, MICRO, q_rows, NOPE_DIM + LANES), bf16),
            pltpu.VMEM((hw, MICRO, q_rows, keys), f32),
            pltpu.VMEM((MICRO, q_rows, keys), bf16),
            pltpu.VMEM((MICRO, q_rows, keys), f32),
            dma((3,)),
            dma((N_COPIES,)),
            dma((N_COPIES,)),
            dma((2, 2)),
            dma((OUT_SLOTS, CHIPS)),
            dma((CHIPS - 1, steps)),
            dma((CHIPS - 1, steps)),
            dma((n_blocks,)),
            dma((n_blocks,)),
        ],
        compiler_params=pltpu.CompilerParams(collective_id=0, has_side_effects=True, vmem_limit_bytes=VMEM_LIMIT),
        name="latent_block",
    )(cq, kv, table, w_qup, w_kvup, w_out)


def solution(mesh):
    tok_spec = P(("dp", "sp"), None)
    idx_spec = P(("dp", "sp"))
    group = mesh.shape["sp"]

    def local_body(x_one, seg_one, pos_one, x_two, seg_two, pos_two, w_qdown, gain_q, w_qup, w_kvdown, gain_kv, w_kvup, w_out):
        rows = x_one.shape[0]
        x_both = jnp.concatenate([x_one, x_two], axis=0)
        pos = jnp.concatenate([pos_one, pos_two])
        seg = jnp.concatenate([seg_one, seg_two])
        kv_raw = jnp.dot(x_both, w_kvdown, preferred_element_type=jnp.float32)
        kv_latent = rms_scale(kv_raw[:, :KV_LAT], gain_kv)
        cos_k, sin_k = rope_tables(pos)
        k_rope = rope_rotate(kv_raw[:, KV_LAT:], cos_k, sin_k).astype(jnp.bfloat16)
        q_latent = rms_scale(jnp.dot(x_both, w_qdown, preferred_element_type=jnp.float32), gain_q)
        meta = jnp.stack([seg, pos // 32, pos % 32], axis=1).astype(jnp.bfloat16)
        meta = jnp.pad(meta, ((0, 0), (0, LANES - ROPE_DIM - 3)))
        packed = jnp.concatenate([kv_latent, k_rope, meta], axis=1).reshape(MICRO, rows, KV_PACK)
        table = jnp.concatenate([cos_k, cos_k, -sin_k, sin_k], axis=1).reshape(MICRO, rows, 2 * ROPE_DIM)
        return latent_block(q_latent.reshape(MICRO, rows, -1), packed, table, w_qup, w_kvup, w_out, group)

    rep = P()
    return jax.shard_map(
        local_body,
        mesh=mesh,
        in_specs=(tok_spec, idx_spec, idx_spec, tok_spec, idx_spec, idx_spec, rep, rep, rep, rep, rep, rep, rep),
        out_specs=(tok_spec, tok_spec),
        check_vma=False,
    )
```

time: 421 us -> 122 us (0.29); the launches traced: 414 us -> 121 us
  matrix products: 217 us -> 12.9 us
  blocking collectives: 111 us -> 0 us
  Pallas kernels: 0 us -> 95.4 us
  other arithmetic: 30.8 us -> 6.41 us
  starting transfers between devices: 17.4 us -> 0 us
  waiting for transfers between devices: 15.5 us -> 0 us
  between operations: 14.5 us -> 0.73 us
    dot_general x16 -> x2, matrix products: 217 us -> 12.9 us  [the longest x1 8.35 us: local_body(): jnp.dot(x_both, w_qdown, preferred_element_type=jnp.float32)]
    pallas_call x0 -> x1, Pallas kernels: none -> 95.4 us  [latent_block(): pl.pallas_call(block_kernel, out_shape=(out, out), in_specs=[vmem] * 3 +...]
    all_gather x2 -> x0, blocking collectives: 61.2 us -> none  [micro_block(): rope_all = lax.all_gather(k_rope, 'sp', axis=0, tiled=True)]
    unnamed x1 -> x0, blocking collectives: 50.1 us -> none
    sub x2 -> x0, other arithmetic: 24.1 us -> none  [head_attention(): jax.nn.softmax(jnp.where(allowed[None], scores * QK_DIM ** (-0.5), -1e+30...]
    all_to_all x2 -> x0, starting transfers between devices: 17.1 us -> none  [micro_block(): tok_out = lax.all_to_all(head_out, 'sp', 0, 1, tiled=True)]
    all_to_all x2 -> x0, waiting for transfers between devices: 14.1 us -> none  [micro_block(): tok_out = lax.all_to_all(head_out, 'sp', 0, 1, tiled=True)]
  transfers between devices with their start and end apart: 6 -> 0, of which waited for: 1 -> 0; matrix products, arithmetic and copies ran while one was open for 33% -> 0% of each run, Pallas kernels for 0% -> 0%
where the time goes in v2:
time: 122 us; the launch traced here: 121 us
  Pallas kernels  95.4 us (78%)
  matrix products  12.9 us (11%)
  other arithmetic  6.41 us (5%)
  local copies, waits for them, and re-layouts  6.04 us (5%)
    pallas_call x1, Pallas kernels, latent_block(): pl.pallas_call(block_kernel, out_shape=(out, out), in_specs=[vmem] * 3 +...  95.4 us
    dot_general x1, matrix products, local_body(): jnp.dot(x_both, w_qdown, preferred_element_type=jnp.float32)  8.35 us
    unnamed x7, local copies, waits for them, and re-layouts  4.58 us
    dot_general x1, matrix products, local_body(): kv_raw = jnp.dot(x_both, w_kvdown, preferred_element_type=jnp.float32)  4.54 us

profile of v2, /device:TPU:97, one launch (start us, length us, event | category | flops | bytes accessed | tf_op | source)
XLA Modules:
  0.0 121.5 jit_solution(6657103750236518795)
XLA Ops:
  0.6 1.0 constant_dynamic-update-slice_fusion.1
  1.6 1.0 constant_dynamic-update-slice_fusion
  2.6 4.5 %fusion.14 = f32[64,576]{1,0:T(8,128)S(1)} fusion(bf16[64,5120]{1,0:T(8,128)(2,1)S(1)} %constant_dynamic-update-slice_fusion, bf16[5120,576]{0,1:T(8,128)(2,1)} %param.22), kind=kOutput, calls=%fused_computation.39 | convolution fusion | flops 377487360 | bytes 6701056 | tf_op jit(solution)/shard_map/dot_general | solution.py:463
  7.4 0.8 add_convert_fusion
  8.2 0.1 fusion.7
  8.3 0.1 copy.25
  8.4 0.1 copy.26
  8.5 0.1 multiply_reduce_fusion.1
  8.7 0.7 convert_element_type.31
  9.4 0.1 multiply_convert_fusion.1
  9.4 0.8 convert_reduce_fusion
  10.2 0.7 convert.22
  10.9 0.7 convert.23
  11.5 0.1 maximum_bitcast_fusion
  11.6 0.1 copy.24
  11.7 0.7 fusion.1
  12.5 0.1 convert_element_type.35
  12.6 0.2 multiply_cosine_fusion
  12.8 0.7 pad_maximum_fusion.tab_ref0
  13.5 8.4 %multiply_reduce_fusion = (f32[64]{0:T(128)S(1)}, f32[64,1536]{1,0:T(8,128)S(1)}) fusion(bf16[64,5120]{1,0:T(8,128)(2,1)S(1)} %constant_dynamic-update-slice_fusion, bf16[5120,1536]{1,0:T(8,128)(2,1)} %param.19), kind=kOutput, calls=%fused_computation.1 | convolution fusion | flops 1006829504 | bytes 16777472 | tf_op jit(solution)/shard_map/dot_general | solution.py:467
  21.8 0.8 multiply_convert_fusion
  22.6 95.4 %latent_block.1 = (bf16[32,5120]{1,0:T(8,128)(2,1)}, bf16[32,5120]{1,0:T(8,128)(2,1)}) custom-call(bf16[2,32,1536]{2,1,0:T(8,128)(2,1)} %bitcast.10, bf16[2,32,640]{2,1,0:T(8,128)(2,1)} %bitcast.11, f32[2,32,128]{2,1,0:T(8,128)} %pad_maximum_fusion.tab_ref0, bf16[1536,24576]{1,0:T(8,128)(2,1)} %wqup_ref.1, bf16[512,32768]{1,0:T(8,128)(2,1)} %wkvup_ref.1, ...), custom_call_target="tpu_custom_call" | custom-call | tf_op jit(solution)/shard_map/latent_block/pallas_call | solution.py:415
  118.0 1.7 %copy.32 = bf16[32,5120]{1,0:T(8,128)(2,1)} copy(bf16[32,5120]{1,0:T(8,128)(2,1)} %get-tuple-element.17) | data formatting | bytes 655360
  119.8 1.7 %copy.33 = bf16[32,5120]{1,0:T(8,128)(2,1)} copy(bf16[32,5120]{1,0:T(8,128)(2,1)} %get-tuple-element.18) | data formatting | bytes 655360
  (11 shorter events, 0.3 us)
Async XLA Ops:
  2.6 19.2 %copy-start = (bf16[1536]{0:T(1024)(128)(2,1)S(1)}, bf16[1536]{0:T(1024)(128)(2,1)}, u32[]{:S(2)}) copy-start(bf16[1536]{0:T(1024)(128)(2,1)} %param.20) | copy-start | bytes 9220

commit v3 on v2

--- a/solution.py
+++ b/solution.py
@@ -2,6 +2,7 @@
 
 import jax
 import jax.numpy as jnp
+import numpy as np
 from jax import lax
 from jax.experimental import pallas as pl
 from jax.experimental.pallas import tpu as pltpu
@@ -26,29 +27,10 @@
 HEADS_PER_STEP = 2
 SOFT_ROWS = 16
 OUT_COLS = 256
-OUT_SLOTS = 7
+OUT_SLOTS = 6
 LAG = 3
 VMEM_LIMIT = 67_043_328
 MESH = pl.DeviceIdType.MESH
-
-
-def rms_scale(pre_norm, gain_vec):
-    mean_sq = jnp.mean(pre_norm * pre_norm, axis=-1, keepdims=True)
-    return (pre_norm * lax.rsqrt(mean_sq + NORM_EPS) * gain_vec.astype(jnp.float32)).astype(jnp.bfloat16)
-
-
-def rope_tables(positions):
-    half_dim = ROPE_DIM // 2
-    inv_freq = ROPE_BASE ** (-jnp.arange(half_dim, dtype=jnp.float32) / half_dim)
-    angles = positions.astype(jnp.float32)[..., None] * inv_freq
-    return jnp.cos(angles), jnp.sin(angles)
-
-
-def rope_rotate(rot_in, cos_tab, sin_tab):
-    half_dim = ROPE_DIM // 2
-    first_half = rot_in[..., :half_dim]
-    second_half = rot_in[..., half_dim:]
-    return jnp.concatenate([first_half * cos_tab - second_half * sin_tab, second_half * cos_tab + first_half * sin_tab], axis=-1)
 
 
 def place():
@@ -105,21 +87,19 @@
         handed.append(send(cq_all.at[slot, 0], cq_all.at[slot, 1], sib))
         handed.append(send(tab_all.at[slot, 0], tab_all.at[slot, 1], sib))
 
-    own = (
-        pltpu.make_async_copy(kv_ref, kv_all.at[me], loc.at[0]),
-        pltpu.make_async_copy(cq_ref, cq_all.at[0, 0], loc.at[1]),
-        pltpu.make_async_copy(tab_ref, tab_all.at[0, 0], loc.at[2]),
-    )
-    for copy in own:
-        copy.start()
+    own = [pltpu.make_async_copy(tab_ref, tab_all.at[0, 0], loc.at[2])]
+    own[0].start()
+    tab_in = {s: send(tab_ref, tab_all.at[s, 0], square[s]) for s in (1, 2, 3)}
+    handed.append(send(tab_ref, tab_all.at[0, 1], sib))
+    yield
+
+    own.append(pltpu.make_async_copy(kv_ref, kv_all.at[me], loc.at[0]))
+    own[1].start()
     first_r = send(kv_ref, kv_all.at[me], right1)
     first_l = send(kv_ref, kv_all.at[me], left1)
     second = {0: (send(kv_ref, kv_all.at[me], right2), send(kv_ref, kv_all.at[me], left2))}
-    tab_in = {s: send(tab_ref, tab_all.at[s, 0], square[s]) for s in (1, 2, 3)}
-    cq_in = {s: send(cq_ref, cq_all.at[s, 0], square[s]) for s in (1, 2)}
     handed.append(send(kv_ref, kv_all.at[me], sib))
-    handed.append(send(cq_ref, cq_all.at[0, 1], sib))
-    handed.append(send(tab_ref, tab_all.at[0, 1], sib))
+    yield
 
     first_r.wait_recv()
     far_r = send_kv(left1, right1, 0)
@@ -129,6 +109,13 @@
     far_l = send_kv(right1, left1, 1)
     second[1] = (send_kv(right1, right2), send_kv(right1, left2))
     hand_kv(right1)
+
+    yield
+
+    own.append(pltpu.make_async_copy(cq_ref, cq_all.at[0, 0], loc.at[1]))
+    own[2].start()
+    cq_in = {s: send(cq_ref, cq_all.at[s, 0], square[s]) for s in (1, 2)}
+    handed.append(send(cq_ref, cq_all.at[0, 1], sib))
 
     def pass_on(first):
         r, l = second[first]
@@ -173,13 +160,15 @@
         copy.wait_send()
     for copy in own:
         copy.wait()
+    yield
 
 
 N_COPIES = 4 + 3 + 2 + 3 + 2 + 4 * 2 + 2 * 3 + 15 + 2 + 6
 
 
 def block_kernel(
-    cq_ref, kv_ref0, tab_ref0, wqup_ref, wkvup_ref, wout_ref, y1_ref, y2_ref,
+    x1_ref, x2_ref, seg1_ref, pos1_ref, seg2_ref, pos2_ref, freq_ref, gq_ref, gkv_ref, wqd_ref, wkvd_ref, wqup_ref, wkvup_ref, wout_ref, y_ref,
+    x_ref, kvd_buf, q_raw, cq_ref, kv_ref0, tab_ref0,
     cq_ref_all, kv_ref, tab_ref, wq_buf, wkv_buf, wo_buf, o_ref, o_in, y_own, y_far, y_in,
     kcat_ref, v_ref, qcat_ref, s_ref, p_ref, mask_ref,
     loc, g_send, g_recv, w_sem, wo_sem, o_send_sem, o_recv_sem, y_send_sem, y_recv_sem,
@@ -225,16 +214,81 @@
             for d in range(CHIPS)
         ]
 
+    depth = wqd_ref.shape[0]
+    part = wo_buf.shape[2]
+    cuts = [(d, d * part, min(part, depth - d * part)) for d in range((depth + part - 1) // part)]
+
+    def down_copies(n):
+        return [
+            pltpu.make_async_copy(
+                wqd_ref.at[at:at + size, n * blk:(n + 1) * blk], wo_buf.at[n, d, 0:size], wo_sem.at[n, d]
+            )
+            for d, at, size in cuts
+        ]
+
+    kv_down = pltpu.make_async_copy(wkvd_ref, kvd_buf, loc.at[3])
+    kv_down.start()
+    q_blocks = q_lat // blk
+    for n in range(q_blocks):
+        for copy in down_copies(n):
+            copy.start()
     for copy in weight_copies(0):
         copy.start()
 
-    @pl.loop(0, slots)
-    def _(b):
-        for copy in out_copies(b):
+
+    def column(ref):
+        square_at = lambda axis: lax.broadcasted_iota(jnp.int32, (rows, rows), axis)
+        spread = jnp.broadcast_to(ref[...].astype(jnp.float32)[None, :], (rows, rows))
+        return jnp.sum(jnp.where(square_at(0) == square_at(1), spread, 0.0), axis=1, keepdims=True)
+
+    lane = lax.broadcasted_iota(jnp.int32, (rows, LANES), 1)
+    tags = []
+    for mb, (seg_in, pos_in) in enumerate(((seg1_ref, pos1_ref), (seg2_ref, pos2_ref))):
+        seg, pos = column(seg_in), column(pos_in)
+        angle = pos * freq_ref[...]
+        sign = jnp.where(lane < ROPE_DIM + ROPE_DIM // 2, -1.0, 1.0)
+        tab_ref0[mb] = jnp.where(lane < ROPE_DIM, jnp.cos(angle), sign * jnp.sin(angle))
+        high = jnp.floor(pos * (1.0 / 32.0))
+        tag = jnp.where(lane == 1, high, jnp.where(lane == 2, pos - 32.0 * high, 0.0))
+        tags.append(jnp.where(lane == 0, seg, tag)[:, :LANES - ROPE_DIM])
+    x_ref[:rows] = x1_ref[...]
+    x_ref[rows:] = x2_ref[...]
+    meet((sib, square[3], near(1, 0), near(-1, 0), near(0, 1), near(0, -1)))
+    flow = gather(where, cq_ref, kv_ref0, tab_ref0, cq_ref_all, kv_ref, tab_ref, loc, g_send, g_recv)
+    next(flow)
+
+    def norm(z, gain):
+        mean_sq = jnp.mean(z * z, axis=-1, keepdims=True)
+        return (z * lax.rsqrt(mean_sq + NORM_EPS) * gain[...].astype(jnp.float32)[None, :]).astype(jnp.bfloat16)
+
+    def turn(z, tab):
+        turned = jnp.concatenate([z[:, ROPE_DIM // 2:], z[:, :ROPE_DIM // 2]], axis=1)
+        return z * tab[:, :ROPE_DIM] + turned * tab[:, ROPE_DIM:]
+
+    kv_down.wait()
+    u = lax.dot_general(x_ref[...], kvd_buf[...], (((1,), (1,)), ((), ())), preferred_element_type=jnp.float32)
+    latent = norm(u[:, :KV_LAT], gkv_ref)
+    k_rope = turn(u[:, KV_LAT:], tab_ref0[...].reshape(MICRO * rows, LANES))
+    packed = jnp.concatenate([latent, jnp.concatenate([k_rope, jnp.concatenate(tags, axis=0)], axis=1).astype(jnp.bfloat16)], axis=1)
+    kv_ref0[...] = packed.reshape(kv_ref0.shape)
+    next(flow)
+    for n in range(q_blocks):
+        for copy in down_copies(n):
+            copy.wait()
+        total = None
+        for d, at, size in cuts:
+            term = jnp.dot(x_ref[:, at:at + size], wo_buf[n, d, 0:size], preferred_element_type=jnp.float32)
+            total = term if total is None else total + term
+        q_raw[:, n * blk:(n + 1) * blk] = total
+        for copy in out_copies(n):
             copy.start()
-
-    meet((sib, square[3], near(1, 0), near(-1, 0), near(0, 1), near(0, -1)))
-    gather(where, cq_ref, kv_ref0, tab_ref0, cq_ref_all, kv_ref, tab_ref, loc, g_send, g_recv)
+        if n == q_blocks - 3:
+            next(flow)
+    for n in range(q_blocks, slots):
+        for copy in out_copies(n):
+            copy.start()
+    cq_ref[...] = norm(q_raw[...], gq_ref).reshape(cq_ref.shape)
+    next(flow)
 
     lane = lax.broadcasted_iota(jnp.int32, (LANES, LANES), 1)
     weight = jnp.where(lane == ROPE_DIM, float(keys), jnp.where(lane == ROPE_DIM + 1, 32.0, jnp.where(lane == ROPE_DIM + 2, 1.0, 0.0)))
@@ -366,8 +420,7 @@
         y_copy(b).wait()
         y = (y_own[b] + y_in[b]).astype(jnp.bfloat16)
         at = pl.ds(pl.multiple_of(b * blk, LANES), blk)
-        y1_ref[:, at] = y[:rows]
-        y2_ref[:, at] = y[rows:]
+        y_ref[:, at] = y
 
     @pl.loop(0, n_blocks)
     def _(b):
@@ -398,29 +451,38 @@
         finish(b)
 
 
-def latent_block(cq, kv, table, w_qup, w_kvup, w_out, group):
-    rows = kv.shape[1]
+def latent_block(x_one, x_two, seg_one, pos_one, seg_two, pos_two, freq, gain_q, gain_kv, w_qdown, w_kvdown, w_qup, w_kvup, w_out, group):
+    rows = x_one.shape[0]
     keys = group * rows
     q_rows = MEMBERS * rows
     hw = HEADS_PER_STEP
+    cq = (MICRO, rows, w_qdown.shape[1])
+    kv = (MICRO, rows, KV_PACK)
+    table = (MICRO, rows, LANES)
     heads = w_out.shape[0] // V_DIM
     steps = heads // MEMBERS // hw
     cols = w_out.shape[1]
     n_blocks = cols // OUT_COLS
-    out = jax.ShapeDtypeStruct((rows, cols), jnp.bfloat16)
+    out = jax.ShapeDtypeStruct((MICRO * rows, cols), jnp.bfloat16)
     dma = pltpu.SemaphoreType.DMA
     vmem, anywhere = pl.BlockSpec(memory_space=pltpu.VMEM), pl.BlockSpec(memory_space=pl.ANY)
     pair = (steps, CORES, MICRO, rows, hw * V_DIM)
     bf16, f32 = jnp.bfloat16, jnp.float32
     return pl.pallas_call(
         block_kernel,
-        out_shape=(out, out),
-        in_specs=[vmem] * 3 + [anywhere] * 3,
-        out_specs=(vmem, vmem),
+        out_shape=out,
+        in_specs=[vmem] * 9 + [anywhere] * 5,
+        out_specs=vmem,
         scratch_shapes=[
-            pltpu.VMEM((CHIPS, CORES) + cq.shape, bf16),
-            pltpu.VMEM((group,) + kv.shape, bf16),
-            pltpu.VMEM((CHIPS, CORES) + table.shape, f32),
+            pltpu.VMEM((MICRO * rows, x_one.shape[1]), bf16),
+            pltpu.VMEM(w_kvdown.shape, bf16),
+            pltpu.VMEM((MICRO * rows, w_qdown.shape[1]), f32),
+            pltpu.VMEM(cq, bf16),
+            pltpu.VMEM(kv, bf16),
+            pltpu.VMEM(table, f32),
+            pltpu.VMEM((CHIPS, CORES) + cq, bf16),
+            pltpu.VMEM((group,) + kv, bf16),
+            pltpu.VMEM((CHIPS, CORES) + table, f32),
             pltpu.VMEM((2, w_qup.shape[0], hw * QK_DIM), bf16),
             pltpu.VMEM((2, w_kvup.shape[0], hw * KV_HEAD), bf16),
             pltpu.VMEM((OUT_SLOTS, CHIPS, heads // MEMBERS * V_DIM, OUT_COLS), bf16),
@@ -435,7 +497,7 @@
             pltpu.VMEM((hw, MICRO, q_rows, keys), f32),
             pltpu.VMEM((MICRO, q_rows, keys), bf16),
             pltpu.VMEM((MICRO, q_rows, keys), f32),
-            dma((3,)),
+            dma((4,)),
             dma((N_COPIES,)),
             dma((N_COPIES,)),
             dma((2, 2)),
@@ -447,7 +509,7 @@
         ],
         compiler_params=pltpu.CompilerParams(collective_id=0, has_side_effects=True, vmem_limit_bytes=VMEM_LIMIT),
         name="latent_block",
-    )(cq, kv, table, w_qup, w_kvup, w_out)
+    )(x_one, x_two, seg_one, pos_one, seg_two, pos_two, freq, gain_q, gain_kv, w_qdown, w_kvdown, w_qup, w_kvup, w_out)
 
 
 def solution(mesh):
@@ -457,19 +519,13 @@
 
     def local_body(x_one, seg_one, pos_one, x_two, seg_two, pos_two, w_qdown, gain_q, w_qup, w_kvdown, gain_kv, w_kvup, w_out):
         rows = x_one.shape[0]
-        x_both = jnp.concatenate([x_one, x_two], axis=0)
-        pos = jnp.concatenate([pos_one, pos_two])
-        seg = jnp.concatenate([seg_one, seg_two])
-        kv_raw = jnp.dot(x_both, w_kvdown, preferred_element_type=jnp.float32)
-        kv_latent = rms_scale(kv_raw[:, :KV_LAT], gain_kv)
-        cos_k, sin_k = rope_tables(pos)
-        k_rope = rope_rotate(kv_raw[:, KV_LAT:], cos_k, sin_k).astype(jnp.bfloat16)
-        q_latent = rms_scale(jnp.dot(x_both, w_qdown, preferred_element_type=jnp.float32), gain_q)
-        meta = jnp.stack([seg, pos // 32, pos % 32], axis=1).astype(jnp.bfloat16)
-        meta = jnp.pad(meta, ((0, 0), (0, LANES - ROPE_DIM - 3)))
-        packed = jnp.concatenate([kv_latent, k_rope, meta], axis=1).reshape(MICRO, rows, KV_PACK)
-        table = jnp.concatenate([cos_k, cos_k, -sin_k, sin_k], axis=1).reshape(MICRO, rows, 2 * ROPE_DIM)
-        return latent_block(q_latent.reshape(MICRO, rows, -1), packed, table, w_qup, w_kvup, w_out, group)
+        half = ROPE_DIM // 2
+        inv_freq = np.float32(ROPE_BASE) ** (-np.arange(half, dtype=np.float32) / half)
+        freq = np.tile(inv_freq, LANES // half)[None, :]
+        y = latent_block(
+            x_one, x_two, seg_one, pos_one, seg_two, pos_two, freq, gain_q, gain_kv, w_qdown, w_kvdown.T, w_qup, w_kvup, w_out, group
+        )
+        return y[:rows], y[rows:]
 
     rep = P()
     return jax.shard_map(

time: 122 us -> 107 us (0.88)
  matrix products: 12.9 us -> 0 us
  Pallas kernels: 95.4 us -> 104 us
  other arithmetic: 6.41 us -> 0 us
  local copies, waits for them, and re-layouts: 6.04 us -> 1.95 us
    dot_general x2 -> x0, matrix products: 12.9 us -> none  [the longest x1 8.35 us: local_body(): jnp.dot(x_both, w_qdown, preferred_element_type=jnp.float32)]
    pallas_call x1, Pallas kernels: 95.4 us -> 104 us  [latent_block(): pl.pallas_call(block_kernel, out_shape=out, in_specs=[vmem] * 9 + [anywhe...]
    unnamed x7 -> x0, local copies, waits for them, and re-layouts: 4.58 us -> none
    convert_element_type x6 -> x0, other arithmetic: 3.08 us -> none  [the longest x2 1.52 us: rope_tables(): angles = positions.astype(jnp.float32)[..., None] * inv_freq]
    slice x1, local copies, waits for them, and re-layouts: 0.07 us -> 1.95 us  [local_body(): return (y[:rows], y[rows:])]
    another operation x6 -> x0, other arithmetic: 1.57 us -> none
    concatenate x2 -> x0, other arithmetic: 1.42 us -> none  [the longest x1 0.72 us: local_body(): jnp.concatenate([kv_latent, k_rope, meta], axis=1)]
where the time goes in v3:
time: 107 us; the launch traced here: 106 us
  Pallas kernels  104 us (97%)
  local copies, waits for them, and re-layouts  1.95 us (2%)
    pallas_call x1, Pallas kernels, latent_block(): pl.pallas_call(block_kernel, out_shape=out, in_specs=[vmem] * 9 + [anywhe...  104 us

profile of v3, /device:TPU:97, one launch (start us, length us, event | category | flops | bytes accessed | tf_op | source)
XLA Modules:
  0.0 106.4 jit_solution(8293553439020519877)
XLA Ops:
  0.6 103.8 %latent_block.1 = bf16[64,5120]{1,0:T(8,128)(2,1)} custom-call(bf16[32,5120]{1,0:T(8,128)(2,1)} %x1_ref.1, bf16[32,5120]{1,0:T(8,128)(2,1)} %x2_ref.1, s32[32]{0:T(128)} %seg1_ref.1, s32[32]{0:T(128)} %pos1_ref.1, s32[32]{0:T(128)} %seg2_ref.1, s32[32]{0:T(128)} %pos2_ref.1, f32[1,128]{1,0:T(1,128)} %constant.2.clone.freq_ref, bf16[1536]{0:T(1024)(128)(2,1)} %gq_ref.1, ...), custom_call_target="tpu_custom_call" | custom-call | tf_op jit(solution)/shard_map/latent_block/pallas_call | solution.py:471
  104.4 1.9 %fusion = (bf16[32,5120]{1,0:T(8,128)(2,1)}, bf16[32,5120]{1,0:T(8,128)(2,1)}) fusion(bf16[64,5120]{1,0:T(8,128)(2,1)} %latent_block.1), kind=kLoop, calls=%fused_computation | loop fusion | bytes 1310720 | tf_op jit(solution)/shard_map/slice | solution.py:528
